TPU v7x, 8 devices: a whole 2x2x1 slice. The times are simulated.
8 devices in a mesh: dp: 1 (over z), sp: 8 (over y, x, core).
Axes of the slice: x: 2, y: 2, z: 1, core: 2. Of those that a mesh axis runs over, the one named last changes fastest.
Arguments:
- hidden: bfloat16 [32, 5120], P('dp')
- ckv_cache: bfloat16 [32, 16384, 512], P('dp', 'sp')
- kpe_cache: bfloat16 [32, 16384, 64], P('dp', 'sp')
- cache_len: int32 [32], P('dp')
- w_dq: bfloat16 [5120, 1536], replicated
- q_gain: bfloat16 [1536], replicated
- w_uq: bfloat16 [1536, 24576], replicated
- w_dkv: bfloat16 [5120, 576], replicated
- kv_gain: bfloat16 [512], replicated
- w_uk: bfloat16 [128, 128, 512], replicated
- w_uv: bfloat16 [128, 128, 512], replicated
- w_out: bfloat16 [16384, 5120], replicated
Outputs:
- output 1: bfloat16 [32, 5120], P('dp')
- output 2: bfloat16 [32, 16384, 512], P('dp', 'sp')
- output 3: bfloat16 [32, 16384, 64], P('dp', 'sp')
- output 4: bfloat16 [32, 576], P('dp')
All inputs are finite; a program needn't handle non-finite values.
Results may differ from a plain program's by a relative error of at most 0.0112942.
Values sent between devices are 32-bit elements.
A program may use at most 1.75 GiB of HBM per device.

v0:
```python
import jax
import jax.numpy as jnp
from jax import lax
from jax.sharding import PartitionSpec as P

EPS = 1e-6
ROPE_THETA = 10000.0
NEG_FILL = -1e30


def rms_norm(vector, norm_gain):
    mean_sq = jnp.mean(vector * vector, axis=-1, keepdims=True)
    return vector * lax.rsqrt(mean_sq + EPS) * norm_gain.astype(jnp.float32)


def rope_tables(cache_len, rope_dim):
    inv_freq = jnp.power(ROPE_THETA, -2.0 * jnp.arange(rope_dim // 2, dtype=jnp.float32) / rope_dim)
    rope_angle = cache_len.astype(jnp.float32)[:, None] * inv_freq[None, :]
    return jnp.cos(rope_angle), jnp.sin(rope_angle)


def rotate(vector, cos_t, sin_t):
    half_dim = vector.shape[-1] // 2
    first_half = vector[..., :half_dim]
    second_half = vector[..., half_dim:]
    return jnp.concatenate([first_half * cos_t - second_half * sin_t, second_half * cos_t + first_half * sin_t], axis=-1)


def project_token(hidden, cache_len, w_dq, q_gain, w_uq, w_dkv, kv_gain, w_uk):
    n_seqs = hidden.shape[0]
    n_heads, nope_dim, value_a7 = w_uk.shape
    qk_dim = w_uq.shape[1] // n_heads
    cq_raw = jnp.dot(hidden, w_dq, preferred_element_type=jnp.float32)
    c_q = rms_norm(cq_raw, q_gain).astype(jnp.bfloat16)
    q_full = jnp.dot(c_q, w_uq, preferred_element_type=jnp.float32).astype(jnp.bfloat16)
    q_full = q_full.reshape(n_seqs, n_heads, qk_dim)
    cos_t, sin_t = rope_tables(cache_len, qk_dim - nope_dim)
    q_pe = rotate(q_full[:, :, nope_dim:].astype(jnp.float32), cos_t[:, None, :], sin_t[:, None, :]).astype(jnp.bfloat16)
    q_lat = jnp.einsum('bhn,hnc->bhc', q_full[:, :, :nope_dim], w_uk, preferred_element_type=jnp.float32).astype(jnp.bfloat16)
    kv_raw = jnp.dot(hidden, w_dkv, preferred_element_type=jnp.float32)
    c_kv = rms_norm(kv_raw[:, :value_a7], kv_gain)
    k_pe = rotate(kv_raw[:, value_a7:], cos_t, sin_t)
    kv_new = jnp.concatenate([c_kv, k_pe], axis=-1).astype(jnp.bfloat16)
    return q_lat, q_pe, kv_new


def local_terms(q_lat, q_pe, ckv_blk, kpe_blk, positions, cache_len, score_scale):
    scores = jnp.einsum('bhc,btc->bht', q_lat, ckv_blk, preferred_element_type=jnp.float32)
    scores = scores + jnp.einsum('bhr,btr->bht', q_pe, kpe_blk, preferred_element_type=jnp.float32)
    is_valid = positions[:, None, :] <= cache_len[:, None, None]
    scores = jnp.where(is_valid, scores * score_scale, NEG_FILL)
    row_peak = jnp.max(scores, axis=-1, keepdims=True)
    weights = jnp.exp(scores - row_peak)
    row_denom = jnp.sum(weights, axis=-1, keepdims=True)
    lat_sum = jnp.einsum('bht,btc->bhc', weights.astype(jnp.bfloat16), ckv_blk, preferred_element_type=jnp.float32)
    return row_peak, row_denom, lat_sum


def output_proj(o_lat, w_uv, w_out):
    n_seqs = o_lat.shape[0]
    o_heads = jnp.einsum('bhc,hvc->bhv', o_lat, w_uv, preferred_element_type=jnp.float32).astype(jnp.bfloat16)
    return jnp.dot(o_heads.reshape(n_seqs, -1), w_out, preferred_element_type=jnp.float32).astype(jnp.bfloat16)


def solution(mesh):
    def local_step(hidden, ckv_blk, kpe_blk, cache_len, w_dq, q_gain, w_uq, w_dkv, kv_gain, w_uk, w_uv, w_out):
        shard_len = ckv_blk.shape[1]
        value_a7 = ckv_blk.shape[2]
        score_scale = (w_uk.shape[1] + kpe_blk.shape[2]) ** -0.5
        q_lat, q_pe, kv_new = project_token(hidden, cache_len, w_dq, q_gain, w_uq, w_dkv, kv_gain, w_uk)
        positions = lax.axis_index('sp') * shard_len + lax.broadcasted_iota(jnp.int32, (1, shard_len), 1)
        new_slot = (positions == cache_len[:, None])[:, :, None]
        ckv_out = jnp.where(new_slot, kv_new[:, None, :value_a7], ckv_blk)
        kpe_out = jnp.where(new_slot, kv_new[:, None, value_a7:], kpe_blk)
        row_peak, row_denom, lat_sum = local_terms(q_lat, q_pe, ckv_out, kpe_out, positions, cache_len, score_scale)
        local_stats = jnp.concatenate([row_peak, row_denom, lat_sum], axis=-1)
        gathered = lax.all_gather(local_stats, 'sp')
        all_peaks = gathered[..., :1]
        factor = jnp.exp(all_peaks - jnp.max(all_peaks, axis=0))
        weight_total = jnp.sum(factor * gathered[..., 1:2], axis=0)
        o_lat = (jnp.sum(factor * gathered[..., 2:], axis=0) / weight_total).astype(jnp.bfloat16)
        out = output_proj(o_lat, w_uv, w_out)
        return out, ckv_out, kpe_out, kv_new

    cache_spec = P('dp', 'sp', None)
    return jax.shard_map(local_step, mesh=mesh, in_specs=(P('dp', None), cache_spec, cache_spec, P('dp'), P(), P(), P(), P(), P(), P(), P(), P()), out_specs=(P('dp', None), cache_spec, cache_spec, P('dp', None)), check_vma=False)
```

profile of v0, /device:TPU:0, one launch (start us, length us, event | category | flops | bytes accessed | tf_op | source)
XLA Modules:
  0.0 678.9 jit_solution(136968554907374493)
XLA Ops:
  8.1 8.3 %multiply_reduce_fusion = (f32[32]{0:T(128)S(1)}, f32[32,1536]{1,0:T(8,128)S(1)}) fusion(bf16[32,5120]{1,0:T(8,128)(2,1)S(1)} %copy-done, bf16[5120,1536]{1,0:T(8,128)(2,1)} %param.16), kind=kOutput, calls=%fused_computation.30 | convolution fusion | flops 503414752 | bytes 16253056 | tf_op jit(solution)/shard_map/dot_general | solution.py:33
  16.5 28.5 %convolution_convert_fusion = bf16[32,24576]{1,0:T(8,128)(2,1)} fusion(bf16[1536,24576]{1,0:T(8,128)(2,1)} %param.18, f32[32,1536]{1,0:T(8,128)S(1)} %get-tuple-element.17, f32[1536]{0:T(1024)S(1)} %convert_element_type.41, f32[32]{0:T(128)S(1)} %add_rsqrt_fusion.1), kind=kOutput, calls=%fused_computation.7 | convolution fusion | flops 2416852992 | bytes 77273216 | tf_op jit(solution)/shard_map/dot_general | solution.py:35
  45.0 3.5 reshape.157
  48.5 1.2 slice.51
  50.0 4.5 fusion.28
  54.7 1.6 copy.34
  56.8 10.6 %convert_bitcast_fusion = bf16[32,128,512]{2,0,1:T(8,128)(2,1)} fusion(bf16[128,128,512]{2,1,0:T(8,128)(2,1)} %param.21, bf16[32,128,128]{2,1,0:T(8,128)(2,1)S(1)} %slice.49), kind=kOutput, calls=%fused_computation.17 | convolution fusion | flops 538968064 | bytes 22020096 | tf_op jit(solution)/shard_map/bhn,hnc->bhc/dot_general | solution.py:39
  67.4 7.5 %broadcast_select_fusion.1 = bf16[32,2048,64]{1,2,0:T(8,128)(2,1)} fusion(bf16[32,2048,64]{1,2,0:T(8,128)(2,1)} %param.14, pred[32,2048]{1,0:T(8,128)(4,1)S(1)} %get-tuple-element.11, bf16[32,64]{1,0:T(8,128)(2,1)S(1)} %pad_maximum_fusion.2), kind=kLoop, calls=%fused_computation.12 | loop fusion | flops 4194304 | bytes 16846848 | tf_op jit(solution)/shard_map/jit(_where)/select_n | solution.py:74
  74.9 44.6 %broadcast_select_fusion = bf16[32,2048,512]{2,1,0:T(8,128)(2,1)} fusion(bf16[32,2048,512]{2,1,0:T(8,128)(2,1)} %param.13, pred[32,2048]{1,0:T(8,128)(4,1)S(1)} %get-tuple-element.11, bf16[32,512]{1,0:T(8,128)(2,1)S(1)} %multiply_convert_fusion.2), kind=kLoop, calls=%fused_computation.2 | loop fusion | flops 33554432 | bytes 134316032 | tf_op jit(solution)/shard_map/jit(_where)/select_n | solution.py:73
  119.8 19.0 %fusion.18 = f32[32,128,2048]{2,1,0:T(8,128)} fusion(bf16[32,2048,64]{1,2,0:T(8,128)(2,1)} %broadcast_select_fusion.1, bf16[32,128,32]{1,2,0:T(8,128)(2,1)S(1)} %get-tuple-element.7, bf16[32,128,32]{1,2,0:T(8,128)(2,1)S(1)} %get-tuple-element.6), kind=kOutput, calls=%fused_computation.23 | convolution fusion | flops 1074790400 | bytes 42467328 | tf_op jit(solution)/shard_map/bhr,btr->bht/dot_general | solution.py:49
  138.8 51.0 %fusion.27 = (f32[32,128]{1,0:T(8,128)S(1)}, f32[32,128,2048]{2,1,0:T(8,128)}) fusion(f32[32,128,2048]{2,1,0:T(8,128)} %fusion.18, bf16[32,2048,512]{2,1,0:T(8,128)(2,1)} %broadcast_select_fusion, bf16[32,128,512]{2,0,1:T(8,128)(2,1)} %convert_bitcast_fusion, pred[32,2048]{1,0:T(8,128)(4,1)S(1)} %get-tuple-element.10), kind=kOutput, calls=%fused_computation.53 | convolution fusion | flops 8623484928 | bytes 138493952 | tf_op jit(solution)/shard_map/bhc,btc->bht/dot_general | solution.py:48
  189.8 13.5 %fusion.2 = f32[32,128]{1,0:T(8,128)S(1)} fusion(f32[32,128,2048]{2,1,0:T(8,128)} %get-tuple-element.19, f32[32,128]{1,0:T(8,128)S(1)} %get-tuple-element.18), kind=kLoop, calls=%fused_computation.6 | loop fusion | flops 16773120 | bytes 33587200 | tf_op jit(solution)/shard_map/reduce_sum | solution.py:54
  203.3 36.4 %fusion.3 = f32[32,128,512]{2,1,0:T(8,128)} fusion(bf16[32,2048,512]{2,1,0:T(8,128)(2,1)} %broadcast_select_fusion, f32[32,128,2048]{2,1,0:T(8,128)} %get-tuple-element.19, f32[32,128]{1,0:T(8,128)S(1)} %get-tuple-element.18), kind=kOutput, calls=%fused_computation.8 | convolution fusion | flops 8606711808 | bytes 109068288 | tf_op jit(solution)/shard_map/bht,btc->bhc/dot_general | solution.py:55
  240.4 2.0 copy.26
  242.4 11.8 %pad_maximum_fusion = f32[32,128,514]{2,1,0:T(8,128)} fusion(f32[32,128,512]{2,1,0:T(8,128)} %fusion.3, f32[32,128,1]{2,1,0:T(8,128)S(1)} %copy.27, f32[32,128,1]{2,1,0:T(8,128)} %copy.26), kind=kLoop, calls=%fused_computation.10 | loop fusion | flops 4210688 | bytes 16842752 | tf_op jit(solution)/shard_map/concatenate | solution.py:76
  254.2 11.0 %copy.28 = f32[32,128,514]{1,0,2:T(8,128)} copy(f32[32,128,514]{2,1,0:T(8,128)} %pad_maximum_fusion) | data formatting | bytes 16842752 | tf_op jit(solution)/shard_map/concatenate | solution.py:76
  265.9 301.8 %all-gather.3.cloned.1.call-done = f32[256,128,514]{1,0,2:T(8,128)} async-done(((f32[32,128,514]{1,0,2:T(8,128)}), f32[256,128,514]{1,0,2:T(8,128)}) %all-gather.3.cloned.1.call-update) | async-done | bytes 67371024 | tf_op jit(solution)/shard_map/all_gather | solution.py:77
  567.7 0.9 slice_reduce_fusion
  568.7 1.0 fusion.22
  569.7 25.2 %fusion = f32[32,128,512]{1,0,2:T(8,128)} fusion(f32[8,32,128,514]{2,1,0,3:T(8,128)} %bitcast.3, f32[8,32,128]{2,1,0:T(8,128)S(1)} %get-tuple-element.5), kind=kLoop, calls=%fused_computation.1 | loop fusion | flops 31457280 | bytes 75628544 | tf_op jit(solution)/shard_map/reduce_sum | solution.py:81
  594.9 10.0 %copy.32 = f32[32,128,512]{2,1,0:T(8,128)} copy(f32[32,128,512]{1,0,2:T(8,128)} %fusion) | data formatting | bytes 16777216
  604.9 3.9 divide_convert_fusion
  608.8 8.3 %fusion.12 = bf16[128,4,8,128]{3,2,1,0:T(8,128)(2,1)S(1)} fusion(bf16[128,128,512]{2,1,0:T(8,128)(2,1)} %param.22, bf16[32,128,512]{2,1,0:T(8,128)(2,1)S(1)} %divide_convert_fusion), kind=kOutput, calls=%fused_computation.19 | convolution fusion | flops 537395200 | bytes 22020096 | tf_op jit(solution)/shard_map/bhc,hvc->bhv/dot_general | solution.py:61
  617.1 54.6 %convolution_convert_fusion.1 = bf16[32,5120]{1,0:T(8,128)(2,1)} fusion(bf16[16384,5120]{1,0:T(8,128)(2,1)} %param.23, bf16[128,4,8,128]{3,2,1,0:T(8,128)(2,1)S(1)} %fusion.12), kind=kOutput, calls=%fused_computation.13 | convolution fusion | flops 5368872960 | bytes 169148416 | tf_op jit(solution)/shard_map/dot_general | solution.py:62
  (35 shorter events, 3.6 us)
Async XLA Ops:
  7.2 1.0 copy-start
  7.2 560.6 %all-gather.3.cloned.1.call-start = ((), (), s32[]{:S(2)}) async-start(), calls=%async_computation | async-start | bytes 75792384 | tf_op jit(solution)/shard_map/all_gather | solution.py:77
  16.4 33.5 %copy-start.7 = (s32[32]{0:T(128)S(1)}, s32[32]{0:T(128)}, u32[]{:S(2)}) copy-start(s32[32]{0:T(128)} %param.15) | copy-start | bytes 388
  16.4 33.5 %copy-start.6 = (bf16[512]{0:T(512)(128)(2,1)S(1)}, bf16[512]{0:T(512)(128)(2,1)}, u32[]{:S(2)}) copy-start(bf16[512]{0:T(512)(128)(2,1)} %param.20) | copy-start | bytes 3076
  56.7 10.7 %copy-start.2 = (bf16[32,32]{1,0:T(8,128)(2,1)}, bf16[32,32]{1,0:T(8,128)(2,1)S(1)}, u32[]{:S(2)}) copy-start(bf16[32,32]{1,0:T(8,128)(2,1)S(1)} %get-tuple-element.14) | copy-start | bytes 6148
  56.7 10.7 %copy-start.4 = (bf16[32,32]{1,0:T(8,128)(2,1)}, bf16[32,32]{1,0:T(8,128)(2,1)S(1)}, u32[]{:S(2)}) copy-start(bf16[32,32]{1,0:T(8,128)(2,1)S(1)} %get-tuple-element.15) | copy-start | bytes 6148
  254.2 11.0 %copy-start.3 = (bf16[32,32]{1,0:T(8,128)(2,1)S(1)}, bf16[32,32]{1,0:T(8,128)(2,1)}, u32[]{:S(2)}) copy-start(bf16[32,32]{1,0:T(8,128)(2,1)} %copy-done.2) | copy-start | bytes 6148
  254.2 11.0 %copy-start.5 = (bf16[32,32]{1,0:T(8,128)(2,1)S(1)}, bf16[32,32]{1,0:T(8,128)(2,1)}, u32[]{:S(2)}) copy-start(bf16[32,32]{1,0:T(8,128)(2,1)} %copy-done.4) | copy-start | bytes 6148
  617.0 54.6 %copy-start.1 = (bf16[32,5120]{1,0:T(8,128)(2,1)S(1)}, bf16[32,5120]{1,0:T(8,128)(2,1)}, u32[]{:S(2)}) copy-start(bf16[32,5120]{1,0:T(8,128)(2,1)} %param.12) | copy-start | bytes 983044
Sparse Core Ops, SparseCore 0:
  265.3 302.3 all-gather.2
where the time goes:
time: 688 us; the launch traced here: 679 us
  waiting for transfers between devices  302 us (44%)
  matrix products  221 us (32%)
  other arithmetic  111 us (16%)
  local copies, waits for them, and re-layouts  30.3 us (4%)
  between operations  14.7 us (2%)
    all_gather x1, waiting for transfers between devices, local_step(): gathered = lax.all_gather(local_stats, 'sp')  302 us
    dot_general x1, matrix products, output_proj(): jnp.dot(o_heads.reshape(n_seqs, -1), w_out, preferred_element_type=jnp.fl...  54.6 us
    dot_general x1, matrix products, local_terms(): jnp.einsum('bhc,btc->bht', q_lat, ckv_blk, preferred_element_type=jnp.flo...  51 us
    select_n x1, other arithmetic, local_step(): ckv_out = jnp.where(new_slot, kv_new[:, None, :value_a7], ckv_blk)  44.6 us
    dot_general x1, matrix products, local_terms(): jnp.einsum('bht,btc->bhc', weights.astype(jnp.bfloat16), ckv_blk, preferr...  36.4 us
    dot_general x1, matrix products, project_token(): jnp.dot(c_q, w_uq, preferred_element_type=jnp.float32).astype(jnp.bfloat16)  28.5 us
    reduce_sum x1, other arithmetic, local_step(): jnp.sum(factor * gathered[..., 2:], axis=0) / weight_total  25.2 us
    dot_general x1, matrix products, local_terms(): jnp.einsum('bhr,btr->bht', q_pe, kpe_blk, preferred_element_type=jnp.floa...  19 us
  transfers between devices with their start and end apart: 1, of which 1 were waited for; matrix products, arithmetic and copies ran while one was open for 0% of the time, Pallas kernels for 0%

commit v1 on v0

v1 whole, which is shorter than its diff:
```python
import functools

import jax
import jax.numpy as jnp
from jax import lax
from jax.experimental import pallas as pl
from jax.experimental.pallas import tpu as pltpu
from jax.sharding import PartitionSpec as P

EPS = 1e-6
ROPE_THETA = 10000.0
NEG_FILL = -1e30
MESH = pl.DeviceIdType.MESH
NBUF = 6
AHEAD = 3
TILE_T = 512
CHUNK = 4


def rms_norm(vector, norm_gain):
    mean_sq = jnp.mean(vector * vector, axis=-1, keepdims=True)
    return vector * lax.rsqrt(mean_sq + EPS) * norm_gain.astype(jnp.float32)


def rope_tables(cache_len, rope_dim):
    inv_freq = jnp.power(ROPE_THETA, -2.0 * jnp.arange(rope_dim // 2, dtype=jnp.float32) / rope_dim)
    rope_angle = cache_len.astype(jnp.float32)[:, None] * inv_freq[None, :]
    return jnp.cos(rope_angle), jnp.sin(rope_angle)


def rotate(vector, cos_t, sin_t):
    half_dim = vector.shape[-1] // 2
    first_half = vector[..., :half_dim]
    second_half = vector[..., half_dim:]
    return jnp.concatenate([first_half * cos_t - second_half * sin_t, second_half * cos_t + first_half * sin_t], axis=-1)


def attend_kernel(n_seqs, shard_len, scale, len_ref, info_ref, qm_ref, qo_ref, pm_ref, po_ref, cnew_ref, knew_ref,
                  ckv_hbm, kpe_hbm, ckv_out, kpe_out, o_ref, lse_ref, cbuf, kbuf, s_scr, lse_scr, in_sem, out_sem):
    step = pl.program_id(0)
    chip = info_ref[1]

    def copies_in(seq):
        slot = lax.rem(seq, NBUF)
        return (pltpu.make_async_copy(ckv_hbm.at[seq], cbuf.at[slot], in_sem.at[0, slot]),
                pltpu.make_async_copy(kpe_hbm.at[seq], kbuf.at[slot], in_sem.at[1, slot]))

    def copies_out(seq):
        slot = lax.rem(seq, NBUF)
        return (pltpu.make_async_copy(cbuf.at[slot], ckv_out.at[seq], out_sem.at[0, slot]),
                pltpu.make_async_copy(kbuf.at[slot], kpe_out.at[seq], out_sem.at[1, slot]))

    @pl.when(step == 0)
    def _():
        for seq in range(AHEAD):
            for copy in copies_in(jnp.int32(seq)):
                copy.start()

    ahead = step + AHEAD

    @pl.when(ahead < n_seqs)
    def _():
        @pl.when(ahead >= NBUF)
        def _():
            for copy in copies_out(ahead - NBUF):
                copy.wait()
        for copy in copies_in(ahead):
            copy.start()

    for copy in copies_in(step):
        copy.wait()
    slot = lax.rem(step, NBUF)
    pos = len_ref[step] - info_ref[0]

    @pl.when((pos >= 0) & (pos < shard_len))
    def _():
        row0 = pl.multiple_of((pos // 16) * 16, 16)
        block = cbuf[slot, pl.ds(row0, 16), :].astype(jnp.float32)
        rows = lax.broadcasted_iota(jnp.int32, block.shape, 0) + row0
        cbuf[slot, pl.ds(row0, 16), :] = jnp.where(rows == pos, cnew_ref[pl.ds(step, 1), :], block).astype(jnp.bfloat16)
        col0 = pl.multiple_of((pos // 128) * 128, 128)
        seq_lane = lax.broadcasted_iota(jnp.int32, knew_ref.shape, 1) == step
        new_col = jnp.sum(jnp.where(seq_lane, knew_ref[...], 0.0), axis=1, keepdims=True)
        kblock = kbuf[slot, :, pl.ds(col0, 128)].astype(jnp.float32)
        cols = lax.broadcasted_iota(jnp.int32, kblock.shape, 1) + col0
        kbuf[slot, :, pl.ds(col0, 128)] = jnp.where(cols == pos, new_col, kblock).astype(jnp.bfloat16)

    q_lat = jnp.concatenate([qm_ref[0], qo_ref[0]], axis=0)
    q_pe = jnp.concatenate([pm_ref[0], po_ref[0]], axis=0)
    peak = None
    for t0 in range(0, shard_len, TILE_T):
        s = lax.dot_general(q_lat, cbuf[slot, t0:t0 + TILE_T, :], (((1,), (1,)), ((), ())), preferred_element_type=jnp.float32)
        s = s + lax.dot_general(q_pe, kbuf[slot, :, t0:t0 + TILE_T], (((1,), (0,)), ((), ())), preferred_element_type=jnp.float32)
        cols = lax.broadcasted_iota(jnp.int32, s.shape, 1) + t0
        s = jnp.where(cols <= pos, s * scale, NEG_FILL)
        s_scr[:, t0:t0 + TILE_T] = s
        tile_peak = jnp.max(s, axis=1, keepdims=True)
        peak = tile_peak if peak is None else jnp.maximum(peak, tile_peak)
    denom = jnp.zeros_like(peak)
    acc = None
    for t0 in range(0, shard_len, TILE_T):
        w = jnp.exp(s_scr[:, t0:t0 + TILE_T] - peak)
        denom = denom + jnp.sum(w, axis=1, keepdims=True)
        part = jnp.dot(w.astype(jnp.bfloat16), cbuf[slot, t0:t0 + TILE_T, :], preferred_element_type=jnp.float32)
        acc = part if acc is None else acc + part
    for copy in copies_out(step):
        copy.start()
    o = acc * (1.0 / denom)
    for half in range(2):
        for group in range(4):
            r0 = half * 64 + group * 16
            o_ref[half, group ^ chip, 0] = o[r0:r0 + 16, :]
    lanes = lax.broadcasted_iota(jnp.int32, lse_scr.shape, 1)
    lse_scr[...] = jnp.where(lanes == step, peak + jnp.log(denom), lse_scr[...])

    @pl.when(step == n_seqs - 1)
    def _():
        lse_ref[...] = jnp.transpose(lse_scr[...])[:n_seqs, :]
        for seq in range(n_seqs - NBUF, n_seqs):
            for copy in copies_out(jnp.int32(seq)):
                copy.wait()


def attend(cache_len, info, q_mine, q_other, pe_mine, pe_other, c_new, k_new, ckv, kpe_t, scale):
    n_seqs, shard_len, lat = ckv.shape
    rope = kpe_t.shape[1]
    per_seq = lambda rows, width: pl.BlockSpec((1, rows, width), lambda i, *_: (i, 0, 0))
    whole = lambda shape: pl.BlockSpec(shape, lambda i, *_: (0,) * len(shape))
    hbm = pl.BlockSpec(memory_space=pl.ANY)
    return pl.pallas_call(
        functools.partial(attend_kernel, n_seqs, shard_len, scale),
        grid_spec=pltpu.PrefetchScalarGridSpec(
            num_scalar_prefetch=2,
            grid=(n_seqs,),
            in_specs=[per_seq(64, lat), per_seq(64, lat), per_seq(64, rope), per_seq(64, rope), whole((n_seqs, lat)),
                      whole((rope, n_seqs)), hbm, hbm],
            out_specs=[hbm, hbm, pl.BlockSpec((2, 4, 1, 16, lat), lambda i, *_: (0, 0, i, 0, 0)), whole((n_seqs, 128))],
            scratch_shapes=[
                pltpu.VMEM((NBUF, shard_len, lat), jnp.bfloat16),
                pltpu.VMEM((NBUF, rope, shard_len), jnp.bfloat16),
                pltpu.VMEM((128, shard_len), jnp.float32),
                pltpu.VMEM((128, 128), jnp.float32),
                pltpu.SemaphoreType.DMA((2, NBUF)),
                pltpu.SemaphoreType.DMA((2, NBUF)),
            ],
        ),
        out_shape=[
            jax.ShapeDtypeStruct(ckv.shape, ckv.dtype),
            jax.ShapeDtypeStruct(kpe_t.shape, kpe_t.dtype),
            jax.ShapeDtypeStruct((2, 4, n_seqs, 16, lat), jnp.float32),
            jax.ShapeDtypeStruct((n_seqs, 128), jnp.float32),
        ],
        compiler_params=pltpu.CompilerParams(dimension_semantics=("arbitrary",), vmem_limit_bytes=60 * 1024 * 1024),
        name="attend",
    )(cache_len, info, q_mine, q_other, pe_mine, pe_other, c_new, k_new, ckv, kpe_t)


def combine_kernel(n_seqs, o_hbm, lse_ref, wuv_hbm, wout_hbm, out_ref, mine, got1, got2, got3, lse_all, w_mine, w_part,
                   wuv, wout, heads, part, part_got, quad, full, load_sem, wt_sem, d1_s, d1_r, s2_s, s2_r, s3_s, s3_r,
                   l_s, l_r, a_s, a_r, b_s, b_r, c_s, c_r, e_s, e_r):
    me = lax.axis_index("sp")
    core = lax.rem(me, 2)
    x_bit = lax.rem(me // 2, 2)
    y_bit = me // 4
    chip = me // 2

    def flip(bits):
        dev = me
        if bits & 1:
            dev = dev + 1 - 2 * core
        if bits & 2:
            dev = dev + 2 - 4 * x_bit
        if bits & 4:
            dev = dev + 4 - 8 * y_bit
        return dev

    def send(src, dst, ssem, rsem, bits):
        return pltpu.make_async_remote_copy(src_ref=src, dst_ref=dst, send_sem=ssem, recv_sem=rsem,
                                            device_id={"sp": flip(bits)}, device_id_type=MESH)

    head0 = core * 64 + chip * 16
    wuv_copy = pltpu.make_async_copy(wuv_hbm.at[pl.ds(head0, 16)], wuv, wt_sem.at[0])
    wout_copy = pltpu.make_async_copy(wout_hbm.at[pl.ds(pl.multiple_of(head0 * 128, 2048), 2048)], wout, wt_sem.at[1])
    n_chunks = n_seqs // CHUNK
    loads = []
    for c in range(n_chunks):
        seqs = pl.ds(c * CHUNK, CHUNK)
        loads.append(pltpu.make_async_copy(o_hbm.at[0, :, seqs], mine.at[:, seqs], load_sem.at[c]))
        loads[c].start()
    wuv_copy.start()
    wout_copy.start()

    barrier = pltpu.get_barrier_semaphore()
    for bits in range(1, 8):
        pl.semaphore_signal(barrier, inc=1, device_id={"sp": flip(bits)}, device_id_type=MESH)
    pl.semaphore_wait(barrier, 7)

    lse_sends = [send(lse_ref, lse_all.at[bits], l_s.at[bits], l_r.at[bits], bits) for bits in range(1, 8)]
    for copy in lse_sends:
        copy.start()
    d1 = []
    for c in range(n_chunks):
        seqs = pl.ds(c * CHUNK, CHUNK)
        d1.append(send(o_hbm.at[1, :, seqs], got1.at[:, seqs], d1_s.at[c], d1_r.at[c], 1))
        d1[c].start()

    for copy in lse_sends:
        copy.wait_recv()
    lses = [lse_ref[...]]
    for bits in range(1, 8):
        other = lse_all[bits]
        lses.append(pltpu.roll(other, 64, 1) if bits & 1 else other)
    peak = functools.reduce(jnp.maximum, lses)
    total = functools.reduce(jnp.add, [jnp.exp(v - peak) for v in lses])
    norm = peak + jnp.log(total)
    pad = jnp.zeros((128 - n_seqs, 128), jnp.float32)
    for value, dst in ((lses[0], w_mine), (lses[1], w_part)):
        wt = jnp.transpose(jnp.concatenate([jnp.exp(value - norm), pad], axis=0))[:64, :]
        for s in range(n_seqs):
            dst[s] = jnp.broadcast_to(wt[:, s:s + 1], (64, 128))

    def orders(c):
        return (1, 2) if c % 2 == 0 else (2, 1)

    s2 = []
    for c in range(n_chunks):
        loads[c].wait()
        d1[c].wait_recv()
        for j in range(4):
            flip_x = x_bit + (1 - 2 * x_bit if j & 1 else 0)
            flip_y = y_bit + (1 - 2 * y_bit if j & 2 else 0)
            row0 = pl.multiple_of((flip_y * 2 + flip_x) * 16, 16)

            def merge(i, _, j=j, row0=row0, c=c):
                s = c * CHUNK + i
                wa = w_mine[s, pl.ds(row0, 16), :]
                wb = w_part[s, pl.ds(row0, 16), :]
                wa = jnp.concatenate([wa] * 4, axis=1)
                wb = jnp.concatenate([wb] * 4, axis=1)
                mine[j, s] = mine[j, s] * wa + got1[j, s] * wb
                return 0

            lax.fori_loop(0, CHUNK, merge, 0)
        first, _ = orders(c)
        seqs = pl.ds(c * CHUNK, CHUNK)
        s2.append((send(mine.at[first, seqs], got2.at[0, seqs], s2_s.at[0, c], s2_r.at[0, c], 2 * first),
                   send(mine.at[3, seqs], got2.at[1, seqs], s2_s.at[1, c], s2_r.at[1, c], 2 * first)))
        for copy in s2[c]:
            copy.start()

    s3 = []
    for c in range(n_chunks):
        _, second = orders(c)
        s2[c][0].wait_recv()
        s2[c][1].wait_recv()

        def add2(i, _, second=second, c=c):
            s = c * CHUNK + i
            mine[second, s] = mine[second, s] + got2[1, s]
            mine[0, s] = mine[0, s] + got2[0, s]
            return 0

        lax.fori_loop(0, CHUNK, add2, 0)
        seqs = pl.ds(c * CHUNK, CHUNK)
        s3.append(send(mine.at[second, seqs], got3.at[seqs], s3_s.at[c], s3_r.at[c], 2 * second))
        s3[c].start()

    for c in range(n_chunks):
        s3[c].wait_recv()

        def add3(i, _, c=c):
            s = c * CHUNK + i
            mine[0, s] = mine[0, s] + got3[s]
            return 0

        lax.fori_loop(0, CHUNK, add3, 0)

    wuv_copy.wait()
    for h in range(16):
        x = mine[0, :, h, :].astype(jnp.bfloat16)
        o = lax.dot_general(x, wuv[h], (((1,), (1,)), ((), ())), preferred_element_type=jnp.float32)
        heads[:, h * 128:(h + 1) * 128] = o.astype(jnp.bfloat16)
    wout_copy.wait()
    width = wout.shape[1] // 8

    for p in range(8):
        part[p // 4, p % 4] = jnp.dot(heads[...], wout[:, p * width:(p + 1) * width], preferred_element_type=jnp.float32)

    a = send(part.at[1 - core], part_got, a_s, a_r, 1)
    a.start()
    a.wait_recv()
    part[core] = part[core] + part_got[...]
    b = []
    for j in range(1, 4):
        flip_x = x_bit + (1 - 2 * x_bit if j & 1 else 0)
        flip_y = y_bit + (1 - 2 * y_bit if j & 2 else 0)
        b.append(send(part.at[core, flip_y * 2 + flip_x], quad.at[j - 1], b_s.at[j - 1], b_r.at[j - 1], 2 * j))
        b[-1].start()
    for copy in b:
        copy.wait_recv()
    done = part[core, chip] + quad[0] + quad[1] + quad[2]
    full[core, chip] = done.astype(jnp.bfloat16).astype(jnp.float32)
    g = [send(full.at[core, chip], full.at[core, chip], c_s.at[j - 1], c_r.at[j - 1], 2 * j) for j in range(1, 4)]
    for copy in g:
        copy.start()
    for copy in g:
        copy.wait_recv()
    e = send(full.at[core], full.at[core], e_s, e_r, 1)
    e.start()
    e.wait_recv()
    for p in range(8):
        out_ref[:, p * width:(p + 1) * width] = full[p // 4, p % 4].astype(jnp.bfloat16)

    for copy in lse_sends + d1 + [c for pair in s2 for c in pair] + s3 + [a] + b + g + [e]:
        copy.wait_send()


def combine(o_parts, lse, w_uv, w_out):
    _, _, n_seqs, _, lat = o_parts.shape
    d_model = w_out.shape[1]
    vdim = w_uv.shape[1]
    n_chunks = n_seqs // CHUNK
    width = d_model // 8
    hbm = pl.BlockSpec(memory_space=pl.ANY)
    vmem = pl.BlockSpec(memory_space=pltpu.VMEM)
    dma = pltpu.SemaphoreType.DMA
    f32 = jnp.float32
    return pl.pallas_call(
        functools.partial(combine_kernel, n_seqs),
        out_shape=jax.ShapeDtypeStruct((n_seqs, d_model), jnp.bfloat16),
        in_specs=[hbm, vmem, hbm, hbm],
        out_specs=vmem,
        scratch_shapes=[
            pltpu.VMEM((4, n_seqs, 16, lat), f32),
            pltpu.VMEM((4, n_seqs, 16, lat), f32),
            pltpu.VMEM((2, n_seqs, 16, lat), f32),
            pltpu.VMEM((n_seqs, 16, lat), f32),
            pltpu.VMEM((8, n_seqs, 128), f32),
            pltpu.VMEM((n_seqs, 64, 128), f32),
            pltpu.VMEM((n_seqs, 64, 128), f32),
            pltpu.VMEM((16, vdim, lat), jnp.bfloat16),
            pltpu.VMEM((16 * vdim, d_model), jnp.bfloat16),
            pltpu.VMEM((n_seqs, 16 * vdim), jnp.bfloat16),
            pltpu.VMEM((2, 4, n_seqs, width), f32),
            pltpu.VMEM((4, n_seqs, width), f32),
            pltpu.VMEM((3, n_seqs, width), f32),
            pltpu.VMEM((2, 4, n_seqs, width), f32),
            dma((n_chunks,)), dma((2,)),
            dma((n_chunks,)), dma((n_chunks,)),
            dma((2, n_chunks)), dma((2, n_chunks)),
            dma((n_chunks,)), dma((n_chunks,)),
            dma((8,)), dma((8,)),
            dma, dma, dma((3,)), dma((3,)), dma((3,)), dma((3,)), dma, dma,
        ],
        compiler_params=pltpu.CompilerParams(collective_id=0, has_side_effects=True, vmem_limit_bytes=60 * 1024 * 1024),
        name="combine",
    )(o_parts, lse, w_uv, w_out)


def solution(mesh):
    def local_step(hidden, ckv_blk, kpe_blk, cache_len, w_dq, q_gain, w_uq, w_dkv, kv_gain, w_uk, w_uv, w_out):
        n_seqs = hidden.shape[0]
        shard_len, lat = ckv_blk.shape[1:]
        n_heads, nope, _ = w_uk.shape
        qk_dim = w_uq.shape[1] // n_heads
        half = n_heads // 2
        scale = (nope + kpe_blk.shape[2]) ** -0.5
        me = lax.axis_index("sp")
        core = me % 2
        cq_raw = jnp.dot(hidden, w_dq, preferred_element_type=jnp.float32)
        c_q = rms_norm(cq_raw, q_gain).astype(jnp.bfloat16)
        w_half = lax.dynamic_slice(w_uq, (0, core * half * qk_dim), (w_uq.shape[0], half * qk_dim))
        q_mine = jnp.dot(c_q, w_half, preferred_element_type=jnp.float32).astype(jnp.bfloat16)
        q_other = lax.ppermute(q_mine.astype(jnp.float32), "sp", [(i, i ^ 1) for i in range(8)])
        cos_t, sin_t = rope_tables(cache_len, qk_dim - nope)

        def finish(q_part, which):
            q_part = q_part.astype(jnp.float32).reshape(n_seqs, half, qk_dim)
            q_pe = rotate(q_part[:, :, nope:], cos_t[:, None, :], sin_t[:, None, :]).astype(jnp.bfloat16)
            uk = lax.dynamic_slice(w_uk, (which * half, 0, 0), (half, nope, lat))
            q_lat = jnp.einsum("bhn,hnc->bhc", q_part[:, :, :nope].astype(jnp.bfloat16), uk, preferred_element_type=jnp.float32)
            return q_lat.astype(jnp.bfloat16), q_pe

        lat_mine, pe_mine = finish(q_mine, core)
        lat_other, pe_other = finish(q_other, 1 - core)
        kv_raw = jnp.dot(hidden, w_dkv, preferred_element_type=jnp.float32)
        c_kv = rms_norm(kv_raw[:, :lat], kv_gain)
        k_pe = rotate(kv_raw[:, lat:], cos_t, sin_t)
        kv_new = jnp.concatenate([c_kv, k_pe], axis=-1).astype(jnp.bfloat16)
        kv_new_f = kv_new.astype(jnp.float32)
        info = jnp.stack([me * shard_len, me // 2]).astype(jnp.int32)
        ckv_out, kpe_out, o_parts, lse = attend(cache_len, info, lat_mine, lat_other, pe_mine, pe_other, kv_new_f[:, :lat],
                                                kv_new_f[:, lat:].T, ckv_blk, jnp.swapaxes(kpe_blk, 1, 2), scale)
        out = combine(o_parts, lse, w_uv, w_out)
        return out, ckv_out, jnp.swapaxes(kpe_out, 1, 2), kv_new

    cache_spec = P("dp", "sp", None)
    return jax.shard_map(local_step, mesh=mesh, in_specs=(P("dp", None), cache_spec, cache_spec, P("dp"), P(), P(), P(), P(), P(), P(), P(), P()), out_specs=(P("dp", None), cache_spec, cache_spec, P("dp", None)), check_vma=False)
```

time: 688 us -> 187 us (0.27); the launches traced: 679 us -> 187 us
  waiting for transfers between devices: 302 us -> 0.01 us
  matrix products: 221 us -> 40.1 us
  Pallas kernels: 0 us -> 126 us
  other arithmetic: 111 us -> 4.28 us
  local copies, waits for them, and re-layouts: 30.3 us -> 15 us
  between operations: 14.7 us -> 0.89 us
    all_gather x1 -> x0, waiting for transfers between devices: 302 us -> none  [local_step(): gathered = lax.all_gather(local_stats, 'sp')]
    dot_general x9 -> x5, matrix products: 221 us -> 40.1 us  [the longest x1 16.3 us: local_step(): jnp.dot(c_q, w_half, preferred_element_type=jnp.float32)]
    pallas_call x0 -> x2, Pallas kernels: none -> 126 us  [the longest x1 66.4 us: combine(): pl.pallas_call(functools.partial(combine_kernel, n_seqs), out_shape=jax.S...]
    select_n x2 -> x0, other arithmetic: 52.1 us -> none  [the longest x1 44.6 us: local_step(): ckv_out = jnp.where(new_slot, kv_new[:, None, :value_a7], ckv_blk)]
    reduce_sum x3 -> x0, other arithmetic: 39.8 us -> none  [the longest x1 25.2 us: local_step(): jnp.sum(factor * gathered[..., 2:], axis=0) / weight_total]
    concatenate x3 -> x2, other arithmetic: 12.6 us -> 1.7 us  [the longest x1 1.62 us: rotate(): jnp.concatenate([first_half * cos_t - second_half * sin_t, second_half *...]
    concatenate x1, local copies, waits for them, and re-layouts: 11 us -> 0.14 us  [local_step(): kv_new = jnp.concatenate([c_kv, k_pe], axis=-1).astype(jnp.bfloat16)]
    unnamed x18 -> x15, local copies, waits for them, and re-layouts: 11.8 us -> 1.99 us
  transfers between devices with their start and end apart: 1 -> 1, of which waited for: 1 -> 0; matrix products, arithmetic and copies ran while one was open for 0% -> 8% of each run, Pallas kernels for 0% -> 0%
where the time goes in v1:
time: 187 us
  Pallas kernels  126 us (67%)
  matrix products  40.1 us (21%)
  local copies, waits for them, and re-layouts  15 us (8%)
  other arithmetic  4.28 us (2%)
    pallas_call x1, Pallas kernels, combine(): pl.pallas_call(functools.partial(combine_kernel, n_seqs), out_shape=jax.S...  66.4 us
    pallas_call x1, Pallas kernels, attend(): pl.pallas_call(functools.partial(attend_kernel, n_seqs, shard_len, scale)...  59.3 us
    dot_general x1, matrix products, local_step(): jnp.dot(c_q, w_half, preferred_element_type=jnp.float32)  16.3 us
    dot_general x2, matrix products, finish(): jnp.einsum('bhn,hnc->bhc', q_part[:, :, :nope].astype(jnp.bfloat16), uk,...  11.1 us
    dot_general x1, matrix products, local_step(): cq_raw = jnp.dot(hidden, w_dq, preferred_element_type=jnp.float32)  8.26 us
    reshape x2, local copies, waits for them, and re-layouts, finish(): q_part = q_part.astype(jnp.float32).reshape(n_seqs, half, qk_dim)  5.56 us
    dot_general x1, matrix products, local_step(): kv_raw = jnp.dot(hidden, w_dkv, preferred_element_type=jnp.float32)  4.47 us
    convert_element_type x1, local copies, waits for them, and re-layouts, finish(): return (q_lat.astype(jnp.bfloat16), q_pe)  4.35 us
  transfers between devices with their start and end apart: 1, of which 0 were waited for; matrix products, arithmetic and copies ran while one was open for 8% of the time, Pallas kernels for 0%

profile of v1, /device:TPU:0, one launch (start us, length us, event | category | flops | bytes accessed | tf_op | source)
XLA Modules:
  0.0 186.9 jit_solution(7958001365665002292)
XLA Ops:
  0.7 0.7 convert_element_type.37
  1.4 0.2 copy-done
  1.6 8.3 %multiply_reduce_fusion = (f32[32]{0:T(128)S(1)}, f32[32,1536]{1,0:T(8,128)S(1)}) fusion(bf16[32,5120]{1,0:T(8,128)(2,1)S(1)} %copy-done, bf16[5120,1536]{1,0:T(8,128)(2,1)} %param.16), kind=kOutput, calls=%fused_computation.23 | convolution fusion | flops 503414752 | bytes 16253056 | tf_op jit(solution)/shard_map/dot_general | solution.py:370
  9.9 16.3 %fusion.5 = f32[32,12288]{1,0:T(8,128)} fusion(bf16[1536,24576]{1,0:T(8,128)(2,1)} %param.18, s32[]{:T(128)S(6)} %select_n.23, f32[32,1536]{1,0:T(8,128)S(1)} %get-tuple-element.27, f32[1536]{0:T(1024)S(1)} %convert_element_type.37, f32[32]{0:T(128)S(1)} %add_rsqrt_fusion.1), kind=kOutput, calls=%fused_computation.3 | convolution fusion | flops 1208893440 | bytes 39524484 | tf_op jit(solution)/shard_map/dot_general | solution.py:373
  26.2 1.0 collective-permute-start
  27.2 4.5 %fusion.21 = f32[32,576]{1,0:T(8,128)S(1)} fusion(bf16[32,5120]{1,0:T(8,128)(2,1)S(1)} %copy-done, bf16[5120,576]{0,1:T(8,128)(2,1)} %param.19), kind=kOutput, calls=%fused_computation.41 | convolution fusion | flops 188743680 | bytes 6299648 | tf_op jit(solution)/shard_map/dot_general | solution.py:386
  31.7 0.1 multiply_reduce_fusion.1
  31.9 0.1 subtract_convert_fusion.2
  32.2 0.1 copy.31
  32.4 2.3 %reshape.82 = f32[32,64,192]{2,1,0:T(8,128)S(1)} reshape(f32[32,12288]{1,0:T(8,128)} %fusion.5) | data formatting | bytes 3145728 | tf_op jit(solution)/shard_map/reshape | solution.py:378
  34.6 0.7 copy.32.cnew_ref
  35.4 0.1 slice.84
  35.5 0.6 pad_add_fusion.info_ref
  36.1 0.6 slice_bitcast_fusion.knew_ref
  36.7 6.1 %fusion.10 = bf16[64,512,32]{1,2,0:T(8,128)(2,1)} fusion(bf16[128,128,512]{2,1,0:T(8,128)(2,1)} %param.21, s32[]{:T(128)S(6)} %select_n.22, bf16[32,64,128]{2,1,0:T(8,128)(2,1)S(1)} %slice.84), kind=kOutput, calls=%fused_computation.6 | convolution fusion | flops 268435456 | bytes 11010052 | tf_op jit(solution)/shard_map/bhn,hnc->bhc/dot_general | solution.py:381
  42.8 3.3 %reshape.83 = f32[32,64,192]{2,1,0:T(8,128)} reshape(f32[32,12288]{1,0:T(8,128)} %collective-permute-done) | data formatting | bytes 3145728 | tf_op jit(solution)/shard_map/reshape | solution.py:378
  46.2 1.5 slice.83
  47.6 5.0 %fusion.8 = bf16[64,512,32]{1,2,0:T(8,128)(2,1)S(1)} fusion(bf16[128,128,512]{2,1,0:T(8,128)(2,1)} %param.21, s32[]{:T(128)S(6)} %select_n.24, bf16[32,64,128]{2,1,0:T(8,128)(2,1)S(1)} %slice.83), kind=kOutput, calls=%fused_computation.4 | convolution fusion | flops 268435456 | bytes 11010052 | tf_op jit(solution)/shard_map/bhn,hnc->bhc/dot_general | solution.py:381
  52.6 0.9 subtract_convert_fusion
  53.5 4.4 %fusion.12 = (bf16[32,64,512]{2,1,0:T(8,128)(2,1)}, bf16[32,64,512]{2,1,0:T(8,128)(2,1)}) fusion(bf16[64,512,32]{1,2,0:T(8,128)(2,1)S(1)} %copy-done.3, bf16[64,512,32]{1,2,0:T(8,128)(2,1)S(1)} %fusion.8), kind=kLoop, calls=%fused_computation.10 | loop fusion | bytes 8388608 | tf_op jit(solution)/shard_map/convert_element_type | solution.py:382
  57.8 1.6 pad_maximum_fusion
  59.5 59.3 %attend.1 = (bf16[32,2048,512]{2,1,0:T(8,128)(2,1)}, bf16[32,64,2048]{2,1,0:T(8,128)(2,1)}, f32[2,4,32,16,512]{4,3,2,1,0:T(8,128)}, f32[32,128]{1,0:T(8,128)}) custom-call(s32[32]{0:T(128)} %len_ref.1, s32[2]{0:T(128)} %pad_add_fusion.info_ref, bf16[32,64,512]{2,1,0:T(8,128)(2,1)} %get-tuple-element.30.qm_ref, ...), custom_call_target="tpu_custom_call" | custom-call | tf_op jit(solution)/shard_map/attend/pallas_call | solution.py:130
  118.8 66.4 %combine.1 = bf16[32,5120]{1,0:T(8,128)(2,1)} custom-call(f32[2,4,32,16,512]{4,3,2,1,0:T(8,128)} %get-tuple-element.8.o_hbm, f32[32,128]{1,0:T(8,128)} %get-tuple-element.9.lse_ref, bf16[128,128,512]{2,1,0:T(8,128)(2,1)} %wuv_hbm.1, bf16[16384,5120]{1,0:T(8,128)(2,1)} %wout_hbm.1), custom_call_target="tpu_custom_call" | custom-call | tf_op jit(solution)/shard_map/combine/pallas_call | solution.py:328
  185.2 1.7 copy.44
  (23 shorter events, 0.3 us)
Async XLA Ops:
  0.6 1.0 copy-start
  9.9 21.8 %copy-start.6 = (s32[32]{0:T(128)S(1)}, s32[32]{0:T(128)}, u32[]{:S(2)}) copy-start(s32[32]{0:T(128)} %len_ref.1) | copy-start | bytes 388
  9.9 21.8 %copy-start.5 = (bf16[512]{0:T(512)(128)(2,1)S(1)}, bf16[512]{0:T(512)(128)(2,1)}, u32[]{:S(2)}) copy-start(bf16[512]{0:T(512)(128)(2,1)} %param.20) | copy-start | bytes 3076
  26.2 16.7 %collective-permute-start = (f32[32,12288]{1,0:T(8,128)}, f32[32,12288]{1,0:T(8,128)}, u32[]{:S(2)}, u32[]{:S(2)}) collective-permute-start(f32[32,12288]{1,0:T(8,128)} %fusion.5), channel_id=1, source_target_pairs={{0,1},{1,0},{2,3},{3,2},{4,5},{5,4},{6,7},{7,6}} | collective-permute-start | bytes 4718600 | tf_op jit(solution)/shard_map/ppermute | solution.py:374
  32.2 10.7 %copy-start.4 = (bf16[32,576]{1,0:T(8,128)(2,1)}, bf16[32,576]{1,0:T(8,128)(2,1)S(1)}, u32[]{:S(2)}) copy-start(bf16[32,576]{1,0:T(8,128)(2,1)S(1)} %pad_maximum_fusion.2) | copy-start | bytes 110596
  46.1 6.5 %copy-start.2 = (f32[32,64,192]{2,1,0:T(8,128)S(1)}, f32[32,64,192]{2,1,0:T(8,128)}, u32[]{:S(2)}) copy-start(f32[32,64,192]{2,1,0:T(8,128)} %reshape.83) | copy-start | bytes 4718596
  47.6 5.9 %copy-start.3 = (bf16[64,512,32]{1,2,0:T(8,128)(2,1)S(1)}, bf16[64,512,32]{1,2,0:T(8,128)(2,1)}, u32[]{:S(2)}) copy-start(bf16[64,512,32]{1,2,0:T(8,128)(2,1)} %fusion.10) | copy-start | bytes 6291460
  118.8 68.2 %copy-start.1 = (bf16[32,5120]{1,0:T(8,128)(2,1)S(1)}, bf16[32,5120]{1,0:T(8,128)(2,1)}, u32[]{:S(2)}) copy-start(bf16[32,5120]{1,0:T(8,128)(2,1)} %param.12) | copy-start | bytes 983044

commit v2 on v1

--- a/solution.py
+++ b/solution.py
@@ -11,15 +11,10 @@
 ROPE_THETA = 10000.0
 NEG_FILL = -1e30
 MESH = pl.DeviceIdType.MESH
-NBUF = 6
-AHEAD = 3
+NBUF = 20
+AHEAD = 10
 TILE_T = 512
 CHUNK = 4
-
-
-def rms_norm(vector, norm_gain):
-    mean_sq = jnp.mean(vector * vector, axis=-1, keepdims=True)
-    return vector * lax.rsqrt(mean_sq + EPS) * norm_gain.astype(jnp.float32)
 
 
 def rope_tables(cache_len, rope_dim):
@@ -28,14 +23,186 @@
     return jnp.cos(rope_angle), jnp.sin(rope_angle)
 
 
-def rotate(vector, cos_t, sin_t):
-    half_dim = vector.shape[-1] // 2
-    first_half = vector[..., :half_dim]
-    second_half = vector[..., half_dim:]
-    return jnp.concatenate([first_half * cos_t - second_half * sin_t, second_half * cos_t + first_half * sin_t], axis=-1)
-
-
-def attend_kernel(n_seqs, shard_len, scale, len_ref, info_ref, qm_ref, qo_ref, pm_ref, po_ref, cnew_ref, knew_ref,
+def project_kernel(n_seqs, hid_ref, qg_ref, kvg_ref, cos_ref, sin_ref, wdq_hbm, wdkv_hbm, wuq_hbm, wuk_hbm,
+                   lat_hbm, pe_hbm, kv_ref, cnew_ref, knew_ref, dq_buf, dkv_buf, uq_buf, uk_buf, q_mine, q_other,
+                   lat_scr, pe_scr, lat_out, pe_out, dq_sem, dkv_sem, uq_sem, uk_sem, lo_sem, po_sem, q_s, q_r):
+    core = lax.rem(lax.axis_index("sp"), 2)
+    partner = lax.axis_index("sp") + 1 - 2 * core
+    f32, bf16 = jnp.float32, jnp.bfloat16
+    n_dq, rows, q_lora = dq_buf.shape
+    tile = uq_buf.shape[2]
+    n_tiles = q_mine.shape[0]
+    lat = lat_scr.shape[2]
+    uq_slots = uq_buf.shape[0]
+    uk_slots = uk_buf.shape[0]
+
+    def uq_copy(i):
+        slot = lax.rem(i, uq_slots)
+        col = pl.multiple_of(core * (n_tiles * tile) + i * tile, tile)
+        return pltpu.make_async_copy(wuq_hbm.at[:, pl.ds(col, tile)], uq_buf.at[slot], uq_sem.at[slot])
+
+    def uk_copy(i):
+        half = i // 4
+        head = (core + half - 2 * core * half) * 64 + lax.rem(i, 4) * 16
+        slot = lax.rem(i, uk_slots)
+        return pltpu.make_async_copy(wuk_hbm.at[pl.ds(head, 16)], uk_buf.at[slot], uk_sem.at[slot])
+
+    dq_copies = [pltpu.make_async_copy(wdq_hbm.at[pl.ds(i * rows, rows)], dq_buf.at[i], dq_sem.at[i]) for i in range(n_dq)]
+    dkv_copy = pltpu.make_async_copy(wdkv_hbm, dkv_buf, dkv_sem)
+    for copy in dq_copies:
+        copy.start()
+    for i in range(uq_slots):
+        uq_copy(jnp.int32(i)).start()
+    dkv_copy.start()
+
+    barrier = pltpu.get_barrier_semaphore()
+    pl.semaphore_signal(barrier, inc=1, device_id={"sp": partner}, device_id_type=MESH)
+    pl.semaphore_wait(barrier, 1)
+
+    def norm(v, gain):
+        mean_sq = jnp.mean(v * v, axis=-1, keepdims=True)
+        return v * lax.rsqrt(mean_sq + EPS) * gain.astype(f32)
+
+    acc = jnp.zeros((n_seqs, q_lora), f32)
+    for i in range(n_dq):
+        dq_copies[i].wait()
+        acc = acc + jnp.dot(hid_ref[:, i * rows:(i + 1) * rows], dq_buf[i], preferred_element_type=f32)
+    c_q = norm(acc, qg_ref[...]).astype(bf16)
+
+    def q_send(i):
+        return pltpu.make_async_remote_copy(src_ref=q_mine.at[i], dst_ref=q_other.at[i], send_sem=q_s.at[i], recv_sem=q_r.at[i],
+                                            device_id={"sp": partner}, device_id_type=MESH)
+
+    def q_tile(i, _):
+        uq_copy(i).wait()
+        q = jnp.dot(c_q, uq_buf[lax.rem(i, uq_slots)], preferred_element_type=f32)
+        q_mine[i] = q.astype(bf16).astype(f32)
+
+        @pl.when(i + uq_slots < n_tiles)
+        def _():
+            uq_copy(i + uq_slots).start()
+
+        @pl.when(i == n_tiles - uq_slots)
+        def _():
+            for k in range(uk_slots):
+                uk_copy(jnp.int32(k)).start()
+
+        @pl.when(i > 0)
+        def _():
+            q_send(i - 1).start()
+        return 0
+
+    lax.fori_loop(0, n_tiles, q_tile, 0)
+    cos_t, sin_t = cos_ref[...], sin_ref[...]
+    lane = lax.broadcasted_iota(jnp.int32, (n_seqs, 128), 1)
+    low_half = lax.rem(lane, 64) < 32
+
+    def rotate_pairs(x):
+        swapped = jnp.where(low_half, pltpu.roll(x, 96, 1), pltpu.roll(x, 32, 1))
+        return x * cos_t + swapped * sin_t
+
+    dkv_copy.wait()
+    kv = lax.dot_general(hid_ref[...], dkv_buf[...], (((1,), (1,)), ((), ())), preferred_element_type=f32)
+    q_send(jnp.int32(n_tiles - 1)).start()
+    c_kv = norm(kv[:, :lat], kvg_ref[...]).astype(bf16)
+    k_raw = jnp.concatenate([kv[:, lat:], jnp.zeros((n_seqs, 64), f32)], axis=1)
+    k_pe = rotate_pairs(k_raw).astype(bf16)
+    kv_ref[:, :lat] = c_kv
+    kv_ref[:, lat:] = k_pe[:, :64]
+    cnew_ref[...] = c_kv.astype(f32)
+    square = jnp.concatenate([k_pe.astype(f32), jnp.zeros((128 - n_seqs, 128), f32)], axis=0)
+    knew_ref[...] = jnp.transpose(square)[:64, :]
+
+    def out_copies(half, g):
+        return (pltpu.make_async_copy(lat_out.at[half, g], lat_hbm.at[half, :, pl.ds(g * 16, 16)], lo_sem.at[half, g]),
+                pltpu.make_async_copy(pe_out.at[half, g], pe_hbm.at[half, :, pl.ds(g * 16, 16)], po_sem.at[half, g]))
+
+    for half in range(2):
+        src = q_mine if half == 0 else q_other
+
+        def group(g, _, half=half, src=src):
+            i = half * 4 + g
+            uk_copy(i).wait()
+            slot = lax.rem(i, uk_slots)
+            if half == 1:
+                q_send(2 * g).wait_recv()
+                q_send(2 * g + 1).wait_recv()
+            for h in range(0, 16, 2):
+                t, p = divmod(h // 2, 4)
+                v = src[2 * g + t, :, p * 384:(p + 1) * 384]
+                even = v[:, :128].astype(bf16)
+                odd = pltpu.roll(v, 192, 1)[:, :128].astype(bf16)
+                x = jnp.where(lane < 64, v[:, 128:256], v[:, 256:384])
+                rot = rotate_pairs(x)
+                pe_scr[:, h, :] = rot
+                pe_scr[:, h + 1, :] = pltpu.roll(rot, 64, 1)
+                lat_scr[:, h, :] = jnp.dot(even, uk_buf[slot, h], preferred_element_type=f32)
+                lat_scr[:, h + 1, :] = jnp.dot(odd, uk_buf[slot, h + 1], preferred_element_type=f32)
+            lat_out[half, g] = lat_scr[...].astype(bf16)
+            pe_out[half, g] = pe_scr[...][:, :, :64].astype(bf16)
+
+            @pl.when(i + uk_slots < 8)
+            def _():
+                uk_copy(i + uk_slots).start()
+            for copy in out_copies(half, g):
+                copy.start()
+            return 0
+
+        lax.fori_loop(0, 4, group, 0)
+
+    def drain(g, _):
+        for half in range(2):
+            for copy in out_copies(half, g):
+                copy.wait()
+        q_send(2 * g).wait_send()
+        q_send(2 * g + 1).wait_send()
+        return 0
+
+    lax.fori_loop(0, 4, drain, 0)
+
+
+def project(hidden, cos_t, sin_t, w_dq, q_gain, w_uq, w_dkv_t, kv_gain, w_uk):
+    n_seqs, d_model = hidden.shape
+    q_lora = w_dq.shape[1]
+    n_heads, nope, lat = w_uk.shape
+    rope = w_uq.shape[1] // n_heads - nope
+    tile = 8 * (nope + rope)
+    n_tiles = n_heads // 16
+    n_dq, uq_slots, uk_slots = 8, 3, 4
+    f32, bf16 = jnp.float32, jnp.bfloat16
+    hbm = pl.BlockSpec(memory_space=pl.ANY)
+    vmem = pl.BlockSpec(memory_space=pltpu.VMEM)
+    dma = pltpu.SemaphoreType.DMA
+    return pl.pallas_call(
+        functools.partial(project_kernel, n_seqs),
+        out_shape=[
+            jax.ShapeDtypeStruct((2, n_seqs, 64, lat), bf16),
+            jax.ShapeDtypeStruct((2, n_seqs, 64, rope), bf16),
+            jax.ShapeDtypeStruct((n_seqs, lat + rope), bf16),
+            jax.ShapeDtypeStruct((n_seqs, lat), f32),
+            jax.ShapeDtypeStruct((rope, 128), f32),
+        ],
+        in_specs=[vmem] * 5 + [hbm] * 4,
+        out_specs=[hbm, hbm, vmem, vmem, vmem],
+        scratch_shapes=[
+            pltpu.VMEM((n_dq, d_model // n_dq, q_lora), bf16),
+            pltpu.VMEM((lat + rope, d_model), bf16),
+            pltpu.VMEM((uq_slots, q_lora, tile), bf16),
+            pltpu.VMEM((uk_slots, 16, nope, lat), bf16),
+            pltpu.VMEM((n_tiles, n_seqs, tile), f32),
+            pltpu.VMEM((n_tiles, n_seqs, tile), f32),
+            pltpu.VMEM((n_seqs, 16, lat), f32),
+            pltpu.VMEM((n_seqs, 16, 128), f32),
+            pltpu.VMEM((2, 4, n_seqs, 16, lat), bf16),
+            pltpu.VMEM((2, 4, n_seqs, 16, rope), bf16),
+            dma((n_dq,)), dma, dma((uq_slots,)), dma((uk_slots,)), dma((2, 4)), dma((2, 4)), dma((n_tiles,)), dma((n_tiles,)),
+        ],
+        compiler_params=pltpu.CompilerParams(collective_id=1, has_side_effects=True, vmem_limit_bytes=60 * 1024 * 1024),
+        name="project",
+    )(hidden, q_gain[None, :], kv_gain[None, :], cos_t, sin_t, w_dq, w_dkv_t, w_uq, w_uk)
+
+
+def attend_kernel(n_seqs, shard_len, scale, len_ref, info_ref, q_ref, pe_ref, cnew_ref, knew_ref,
                   ckv_hbm, kpe_hbm, ckv_out, kpe_out, o_ref, lse_ref, cbuf, kbuf, s_scr, lse_scr, in_sem, out_sem):
     step = pl.program_id(0)
     chip = info_ref[1]
@@ -85,8 +252,8 @@
         cols = lax.broadcasted_iota(jnp.int32, kblock.shape, 1) + col0
         kbuf[slot, :, pl.ds(col0, 128)] = jnp.where(cols == pos, new_col, kblock).astype(jnp.bfloat16)
 
-    q_lat = jnp.concatenate([qm_ref[0], qo_ref[0]], axis=0)
-    q_pe = jnp.concatenate([pm_ref[0], po_ref[0]], axis=0)
+    q_lat = jnp.concatenate([q_ref[0, 0], q_ref[1, 0]], axis=0)
+    q_pe = jnp.concatenate([pe_ref[0, 0], pe_ref[1, 0]], axis=0)
     peak = None
     for t0 in range(0, shard_len, TILE_T):
         s = lax.dot_general(q_lat, cbuf[slot, t0:t0 + TILE_T, :], (((1,), (1,)), ((), ())), preferred_element_type=jnp.float32)
@@ -121,10 +288,10 @@
                 copy.wait()
 
 
-def attend(cache_len, info, q_mine, q_other, pe_mine, pe_other, c_new, k_new, ckv, kpe_t, scale):
+def attend(cache_len, info, q_lat, q_pe, c_new, k_new, ckv, kpe_t, scale):
     n_seqs, shard_len, lat = ckv.shape
     rope = kpe_t.shape[1]
-    per_seq = lambda rows, width: pl.BlockSpec((1, rows, width), lambda i, *_: (i, 0, 0))
+    per_seq = lambda width: pl.BlockSpec((2, 1, 64, width), lambda i, *_: (0, i, 0, 0))
     whole = lambda shape: pl.BlockSpec(shape, lambda i, *_: (0,) * len(shape))
     hbm = pl.BlockSpec(memory_space=pl.ANY)
     return pl.pallas_call(
@@ -132,8 +299,7 @@
         grid_spec=pltpu.PrefetchScalarGridSpec(
             num_scalar_prefetch=2,
             grid=(n_seqs,),
-            in_specs=[per_seq(64, lat), per_seq(64, lat), per_seq(64, rope), per_seq(64, rope), whole((n_seqs, lat)),
-                      whole((rope, n_seqs)), hbm, hbm],
+            in_specs=[per_seq(lat), per_seq(rope), whole((n_seqs, lat)), whole((rope, 128)), hbm, hbm],
             out_specs=[hbm, hbm, pl.BlockSpec((2, 4, 1, 16, lat), lambda i, *_: (0, 0, i, 0, 0)), whole((n_seqs, 128))],
             scratch_shapes=[
                 pltpu.VMEM((NBUF, shard_len, lat), jnp.bfloat16),
@@ -152,7 +318,7 @@
         ],
         compiler_params=pltpu.CompilerParams(dimension_semantics=("arbitrary",), vmem_limit_bytes=60 * 1024 * 1024),
         name="attend",
-    )(cache_len, info, q_mine, q_other, pe_mine, pe_other, c_new, k_new, ckv, kpe_t)
+    )(cache_len, info, q_lat, q_pe, c_new, k_new, ckv, kpe_t)
 
 
 def combine_kernel(n_seqs, o_hbm, lse_ref, wuv_hbm, wout_hbm, out_ref, mine, got1, got2, got3, lse_all, w_mine, w_part,
@@ -359,38 +525,16 @@
 
 def solution(mesh):
     def local_step(hidden, ckv_blk, kpe_blk, cache_len, w_dq, q_gain, w_uq, w_dkv, kv_gain, w_uk, w_uv, w_out):
-        n_seqs = hidden.shape[0]
-        shard_len, lat = ckv_blk.shape[1:]
-        n_heads, nope, _ = w_uk.shape
-        qk_dim = w_uq.shape[1] // n_heads
-        half = n_heads // 2
-        scale = (nope + kpe_blk.shape[2]) ** -0.5
+        shard_len = ckv_blk.shape[1]
+        rope = kpe_blk.shape[2]
+        scale = (w_uk.shape[1] + rope) ** -0.5
         me = lax.axis_index("sp")
-        core = me % 2
-        cq_raw = jnp.dot(hidden, w_dq, preferred_element_type=jnp.float32)
-        c_q = rms_norm(cq_raw, q_gain).astype(jnp.bfloat16)
-        w_half = lax.dynamic_slice(w_uq, (0, core * half * qk_dim), (w_uq.shape[0], half * qk_dim))
-        q_mine = jnp.dot(c_q, w_half, preferred_element_type=jnp.float32).astype(jnp.bfloat16)
-        q_other = lax.ppermute(q_mine.astype(jnp.float32), "sp", [(i, i ^ 1) for i in range(8)])
-        cos_t, sin_t = rope_tables(cache_len, qk_dim - nope)
-
-        def finish(q_part, which):
-            q_part = q_part.astype(jnp.float32).reshape(n_seqs, half, qk_dim)
-            q_pe = rotate(q_part[:, :, nope:], cos_t[:, None, :], sin_t[:, None, :]).astype(jnp.bfloat16)
-            uk = lax.dynamic_slice(w_uk, (which * half, 0, 0), (half, nope, lat))
-            q_lat = jnp.einsum("bhn,hnc->bhc", q_part[:, :, :nope].astype(jnp.bfloat16), uk, preferred_element_type=jnp.float32)
-            return q_lat.astype(jnp.bfloat16), q_pe
-
-        lat_mine, pe_mine = finish(q_mine, core)
-        lat_other, pe_other = finish(q_other, 1 - core)
-        kv_raw = jnp.dot(hidden, w_dkv, preferred_element_type=jnp.float32)
-        c_kv = rms_norm(kv_raw[:, :lat], kv_gain)
-        k_pe = rotate(kv_raw[:, lat:], cos_t, sin_t)
-        kv_new = jnp.concatenate([c_kv, k_pe], axis=-1).astype(jnp.bfloat16)
-        kv_new_f = kv_new.astype(jnp.float32)
+        cos_t, sin_t = rope_tables(cache_len, rope)
+        cos_t = jnp.concatenate([cos_t] * 4, axis=1)
+        sin_t = jnp.concatenate([-sin_t, sin_t] * 2, axis=1)
+        q_lat, q_pe, kv_new, c_new, k_new = project(hidden, cos_t, sin_t, w_dq, q_gain, w_uq, w_dkv.T, kv_gain, w_uk)
         info = jnp.stack([me * shard_len, me // 2]).astype(jnp.int32)
-        ckv_out, kpe_out, o_parts, lse = attend(cache_len, info, lat_mine, lat_other, pe_mine, pe_other, kv_new_f[:, :lat],
-                                                kv_new_f[:, lat:].T, ckv_blk, jnp.swapaxes(kpe_blk, 1, 2), scale)
+        ckv_out, kpe_out, o_parts, lse = attend(cache_len, info, q_lat, q_pe, c_new, k_new, ckv_blk, jnp.swapaxes(kpe_blk, 1, 2), scale)
         out = combine(o_parts, lse, w_uv, w_out)
         return out, ckv_out, jnp.swapaxes(kpe_out, 1, 2), kv_new
 

time: 187 us -> 169 us (0.904)
  matrix products: 40.1 us -> 0 us
  Pallas kernels: 126 us -> 161 us
  local copies, waits for them, and re-layouts: 15 us -> 4.89 us
  other arithmetic: 4.28 us -> 2.11 us
    dot_general x5 -> x0, matrix products: 40.1 us -> none  [the longest x1 16.3 us: local_step(): jnp.dot(c_q, w_half, preferred_element_type=jnp.float32)]
    pallas_call x0 -> x1, Pallas kernels: none -> 30.1 us  [project(): pl.pallas_call(functools.partial(project_kernel, n_seqs), out_shape=[jax....]
    reshape x2 -> x0, local copies, waits for them, and re-layouts: 5.56 us -> none  [finish(): q_part = q_part.astype(jnp.float32).reshape(n_seqs, half, qk_dim)]
    convert_element_type x1 -> x0, local copies, waits for them, and re-layouts: 4.35 us -> none  [finish(): return (q_lat.astype(jnp.bfloat16), q_pe)]
    pallas_call x1, Pallas kernels: 59.3 us -> 63.5 us  [attend(): pl.pallas_call(functools.partial(attend_kernel, n_seqs, shard_len, scale)...]
    broadcast_in_dim x0 -> x2, local copies, waits for them, and re-layouts: none -> 2.55 us  [the longest x1 1.28 us: project(): q_gain[None, :]]
    slice x4 -> x0, local copies, waits for them, and re-layouts: 2.3 us -> none  [the longest x2 1.53 us: finish(): q_part[:, :, :nope].astype(jnp.bfloat16)]
  transfers between devices with their start and end apart: 1 -> 0, of which waited for: 0 -> 0; matrix products, arithmetic and copies ran while one was open for 8% -> 0% of each run, Pallas kernels for 0% -> 0%
where the time goes in v2:
time: 169 us; the launch traced here: 168 us
  Pallas kernels  161 us (95%)
  local copies, waits for them, and re-layouts  4.89 us (3%)
  other arithmetic  2.11 us (1%)
    pallas_call x1, Pallas kernels, combine(): pl.pallas_call(functools.partial(combine_kernel, n_seqs), out_shape=jax.S...  67 us
    pallas_call x1, Pallas kernels, attend(): pl.pallas_call(functools.partial(attend_kernel, n_seqs, shard_len, scale)...  63.5 us
    pallas_call x1, Pallas kernels, project(): pl.pallas_call(functools.partial(project_kernel, n_seqs), out_shape=[jax....  30.1 us

profile of v2, /device:TPU:0, one launch (start us, length us, event | category | flops | bytes accessed | tf_op | source)
XLA Modules:
  0.0 168.2 jit_solution(7182902588927562164)
XLA Ops:
  0.6 0.6 pad_add_fusion.info_ref
  1.2 0.7 convert_element_type.3
  1.9 1.3 broadcast_in_dim.9.kvg_ref
  3.2 1.3 broadcast_in_dim.8.qg_ref
  4.4 0.1 fusion
  4.6 0.7 pad_maximum_fusion
  5.3 30.1 %project.1 = (bf16[2,32,64,512]{3,2,1,0:T(8,128)(2,1)}, bf16[2,32,64,64]{3,2,1,0:T(8,128)(2,1)}, bf16[32,576]{1,0:T(8,128)(2,1)}, f32[32,512]{1,0:T(8,128)}, f32[64,128]{1,0:T(8,128)}) custom-call(bf16[32,5120]{1,0:T(8,128)(2,1)} %hid_ref.1, bf16[1,1536]{1,0:T(2,128)(2,1)} %broadcast_in_dim.8.qg_ref, bf16[1,512]{1,0:T(2,128)(2,1)} %broadcast_in_dim.9.kvg_ref, ...), custom_call_target="tpu_custom_call" | custom-call | tf_op jit(solution)/shard_map/project/pallas_call | solution.py:176
  35.4 63.5 %attend.1 = (bf16[32,2048,512]{2,1,0:T(8,128)(2,1)}, bf16[32,64,2048]{2,1,0:T(8,128)(2,1)}, f32[2,4,32,16,512]{4,3,2,1,0:T(8,128)}, f32[32,128]{1,0:T(8,128)}) custom-call(s32[32]{0:T(128)} %len_ref.1, s32[2]{0:T(128)} %pad_add_fusion.info_ref, bf16[2,32,64,512]{3,2,1,0:T(8,128)(2,1)} %get-tuple-element.13.q_ref, ...), custom_call_target="tpu_custom_call" | custom-call | tf_op jit(solution)/shard_map/attend/pallas_call | solution.py:297
  98.9 0.0 copy-start
  98.9 67.0 %combine.1 = bf16[32,5120]{1,0:T(8,128)(2,1)} custom-call(f32[2,4,32,16,512]{4,3,2,1,0:T(8,128)} %get-tuple-element.17.o_hbm, f32[32,128]{1,0:T(8,128)} %get-tuple-element.18.lse_ref, bf16[128,128,512]{2,1,0:T(8,128)(2,1)} %wuv_hbm.1, bf16[16384,5120]{1,0:T(8,128)(2,1)} %wout_hbm.1), custom_call_target="tpu_custom_call" | custom-call | tf_op jit(solution)/shard_map/combine/pallas_call | solution.py:494
  165.9 1.7 %copy.18 = bf16[32,5120]{1,0:T(8,128)(2,1)} copy(bf16[32,5120]{1,0:T(8,128)(2,1)} %combine.1) | data formatting | bytes 655360
  167.6 0.0 copy-done
  167.6 0.6 copy.19
  (1 shorter events, 0.0 us)
Async XLA Ops:
  98.9 68.8 %copy-start = (bf16[32,576]{1,0:T(8,128)(2,1)S(1)}, bf16[32,576]{1,0:T(8,128)(2,1)}, u32[]{:S(2)}) copy-start(bf16[32,576]{1,0:T(8,128)(2,1)} %get-tuple-element.34) | copy-start | bytes 110596

commit v3 on v2

--- a/solution.py
+++ b/solution.py
@@ -11,8 +11,9 @@
 ROPE_THETA = 10000.0
 NEG_FILL = -1e30
 MESH = pl.DeviceIdType.MESH
-NBUF = 20
-AHEAD = 10
+NBUF = 12
+AHEAD = 6
+OBUF = 4
 TILE_T = 512
 CHUNK = 4
 
@@ -202,20 +203,27 @@
     )(hidden, q_gain[None, :], kv_gain[None, :], cos_t, sin_t, w_dq, w_dkv_t, w_uq, w_uk)
 
 
-def attend_kernel(n_seqs, shard_len, scale, len_ref, info_ref, q_ref, pe_ref, cnew_ref, knew_ref,
-                  ckv_hbm, kpe_hbm, ckv_out, kpe_out, o_ref, lse_ref, cbuf, kbuf, s_scr, lse_scr, in_sem, out_sem):
+def attend_kernel(n_seqs, shard_len, scale, len_ref, cnew_ref, knew_ref, q_hbm, pe_hbm, ckv_hbm, kpe_hbm,
+                  ckv_out, kpe_out, o_hbm, lse_ref, cbuf, kbuf, qbuf, pbuf, obuf, s_scr, lse_scr, in_sem, out_sem, o_sem):
     step = pl.program_id(0)
-    chip = info_ref[1]
+    me = lax.axis_index("sp")
+    chip = me // 2
 
     def copies_in(seq):
         slot = lax.rem(seq, NBUF)
-        return (pltpu.make_async_copy(ckv_hbm.at[seq], cbuf.at[slot], in_sem.at[0, slot]),
-                pltpu.make_async_copy(kpe_hbm.at[seq], kbuf.at[slot], in_sem.at[1, slot]))
+        return (pltpu.make_async_copy(q_hbm.at[:, seq], qbuf.at[slot], in_sem.at[2, slot]),
+                pltpu.make_async_copy(pe_hbm.at[:, seq], pbuf.at[slot], in_sem.at[3, slot]),
+                pltpu.make_async_copy(kpe_hbm.at[seq], kbuf.at[slot], in_sem.at[1, slot]),
+                pltpu.make_async_copy(ckv_hbm.at[seq], cbuf.at[slot], in_sem.at[0, slot]))
 
     def copies_out(seq):
         slot = lax.rem(seq, NBUF)
         return (pltpu.make_async_copy(cbuf.at[slot], ckv_out.at[seq], out_sem.at[0, slot]),
                 pltpu.make_async_copy(kbuf.at[slot], kpe_out.at[seq], out_sem.at[1, slot]))
+
+    def copy_o(seq):
+        slot = lax.rem(seq, OBUF)
+        return pltpu.make_async_copy(obuf.at[slot], o_hbm.at[:, :, seq], o_sem.at[slot])
 
     @pl.when(step == 0)
     def _():
@@ -237,7 +245,7 @@
     for copy in copies_in(step):
         copy.wait()
     slot = lax.rem(step, NBUF)
-    pos = len_ref[step] - info_ref[0]
+    pos = len_ref[step] - me * shard_len
 
     @pl.when((pos >= 0) & (pos < shard_len))
     def _():
@@ -252,8 +260,8 @@
         cols = lax.broadcasted_iota(jnp.int32, kblock.shape, 1) + col0
         kbuf[slot, :, pl.ds(col0, 128)] = jnp.where(cols == pos, new_col, kblock).astype(jnp.bfloat16)
 
-    q_lat = jnp.concatenate([q_ref[0, 0], q_ref[1, 0]], axis=0)
-    q_pe = jnp.concatenate([pe_ref[0, 0], pe_ref[1, 0]], axis=0)
+    q_lat = jnp.concatenate([qbuf[slot, 0], qbuf[slot, 1]], axis=0)
+    q_pe = jnp.concatenate([pbuf[slot, 0], pbuf[slot, 1]], axis=0)
     peak = None
     for t0 in range(0, shard_len, TILE_T):
         s = lax.dot_general(q_lat, cbuf[slot, t0:t0 + TILE_T, :], (((1,), (1,)), ((), ())), preferred_element_type=jnp.float32)
@@ -273,10 +281,16 @@
     for copy in copies_out(step):
         copy.start()
     o = acc * (1.0 / denom)
+    oslot = lax.rem(step, OBUF)
+
+    @pl.when(step >= OBUF)
+    def _():
+        copy_o(step - OBUF).wait()
     for half in range(2):
         for group in range(4):
             r0 = half * 64 + group * 16
-            o_ref[half, group ^ chip, 0] = o[r0:r0 + 16, :]
+            obuf[oslot, half, group ^ chip] = o[r0:r0 + 16, :]
+    copy_o(step).start()
     lanes = lax.broadcasted_iota(jnp.int32, lse_scr.shape, 1)
     lse_scr[...] = jnp.where(lanes == step, peak + jnp.log(denom), lse_scr[...])
 
@@ -286,28 +300,33 @@
         for seq in range(n_seqs - NBUF, n_seqs):
             for copy in copies_out(jnp.int32(seq)):
                 copy.wait()
-
-
-def attend(cache_len, info, q_lat, q_pe, c_new, k_new, ckv, kpe_t, scale):
+        for seq in range(n_seqs - OBUF, n_seqs):
+            copy_o(jnp.int32(seq)).wait()
+
+
+def attend(cache_len, q_lat, q_pe, c_new, k_new, ckv, kpe_t, scale):
     n_seqs, shard_len, lat = ckv.shape
     rope = kpe_t.shape[1]
-    per_seq = lambda width: pl.BlockSpec((2, 1, 64, width), lambda i, *_: (0, i, 0, 0))
     whole = lambda shape: pl.BlockSpec(shape, lambda i, *_: (0,) * len(shape))
     hbm = pl.BlockSpec(memory_space=pl.ANY)
     return pl.pallas_call(
         functools.partial(attend_kernel, n_seqs, shard_len, scale),
         grid_spec=pltpu.PrefetchScalarGridSpec(
-            num_scalar_prefetch=2,
+            num_scalar_prefetch=1,
             grid=(n_seqs,),
-            in_specs=[per_seq(lat), per_seq(rope), whole((n_seqs, lat)), whole((rope, 128)), hbm, hbm],
-            out_specs=[hbm, hbm, pl.BlockSpec((2, 4, 1, 16, lat), lambda i, *_: (0, 0, i, 0, 0)), whole((n_seqs, 128))],
+            in_specs=[whole((n_seqs, lat)), whole((rope, 128)), hbm, hbm, hbm, hbm],
+            out_specs=[hbm, hbm, hbm, whole((n_seqs, 128))],
             scratch_shapes=[
                 pltpu.VMEM((NBUF, shard_len, lat), jnp.bfloat16),
                 pltpu.VMEM((NBUF, rope, shard_len), jnp.bfloat16),
+                pltpu.VMEM((NBUF, 2, 64, lat), jnp.bfloat16),
+                pltpu.VMEM((NBUF, 2, 64, rope), jnp.bfloat16),
+                pltpu.VMEM((OBUF, 2, 4, 16, lat), jnp.float32),
                 pltpu.VMEM((128, shard_len), jnp.float32),
                 pltpu.VMEM((128, 128), jnp.float32),
+                pltpu.SemaphoreType.DMA((4, NBUF)),
                 pltpu.SemaphoreType.DMA((2, NBUF)),
-                pltpu.SemaphoreType.DMA((2, NBUF)),
+                pltpu.SemaphoreType.DMA((OBUF,)),
             ],
         ),
         out_shape=[
@@ -318,7 +337,7 @@
         ],
         compiler_params=pltpu.CompilerParams(dimension_semantics=("arbitrary",), vmem_limit_bytes=60 * 1024 * 1024),
         name="attend",
-    )(cache_len, info, q_lat, q_pe, c_new, k_new, ckv, kpe_t)
+    )(cache_len, c_new, k_new, q_lat, q_pe, ckv, kpe_t)
 
 
 def combine_kernel(n_seqs, o_hbm, lse_ref, wuv_hbm, wout_hbm, out_ref, mine, got1, got2, got3, lse_all, w_mine, w_part,
@@ -339,6 +358,9 @@
         if bits & 4:
             dev = dev + 4 - 8 * y_bit
         return dev
+
+    def flip_chip(j):
+        return (y_bit + (1 - 2 * y_bit if j & 2 else 0)) * 2 + x_bit + (1 - 2 * x_bit if j & 1 else 0)
 
     def send(src, dst, ssem, rsem, bits):
         return pltpu.make_async_remote_copy(src_ref=src, dst_ref=dst, send_sem=ssem, recv_sem=rsem,
@@ -393,9 +415,7 @@
         loads[c].wait()
         d1[c].wait_recv()
         for j in range(4):
-            flip_x = x_bit + (1 - 2 * x_bit if j & 1 else 0)
-            flip_y = y_bit + (1 - 2 * y_bit if j & 2 else 0)
-            row0 = pl.multiple_of((flip_y * 2 + flip_x) * 16, 16)
+            row0 = pl.multiple_of(flip_chip(j) * 16, 16)
 
             def merge(i, _, j=j, row0=row0, c=c):
                 s = c * CHUNK + i
@@ -449,19 +469,26 @@
     wout_copy.wait()
     width = wout.shape[1] // 8
 
-    for p in range(8):
-        part[p // 4, p % 4] = jnp.dot(heads[...], wout[:, p * width:(p + 1) * width], preferred_element_type=jnp.float32)
-
-    a = send(part.at[1 - core], part_got, a_s, a_r, 1)
-    a.start()
-    a.wait_recv()
-    part[core] = part[core] + part_got[...]
+    def project_block(which, order):
+        idx = flip_chip(order)
+        col = pl.multiple_of((which * 4 + idx) * width, 128)
+        part[which, idx] = jnp.dot(heads[...], wout[:, pl.ds(col, width)], preferred_element_type=jnp.float32)
+
+    a = []
+    for j in (3, 1, 2, 0):
+        project_block(1 - core, j)
+        idx = flip_chip(j)
+        a.append(send(part.at[1 - core, idx], part_got.at[j], a_s.at[j], a_r.at[j], 1))
+        a[-1].start()
     b = []
-    for j in range(1, 4):
-        flip_x = x_bit + (1 - 2 * x_bit if j & 1 else 0)
-        flip_y = y_bit + (1 - 2 * y_bit if j & 2 else 0)
-        b.append(send(part.at[core, flip_y * 2 + flip_x], quad.at[j - 1], b_s.at[j - 1], b_r.at[j - 1], 2 * j))
-        b[-1].start()
+    for n, j in enumerate((3, 1, 2, 0)):
+        project_block(core, j)
+        idx = flip_chip(j)
+        a[n].wait_recv()
+        part[core, idx] = part[core, idx] + part_got[j]
+        if j:
+            b.append(send(part.at[core, idx], quad.at[j - 1], b_s.at[j - 1], b_r.at[j - 1], 2 * j))
+            b[-1].start()
     for copy in b:
         copy.wait_recv()
     done = part[core, chip] + quad[0] + quad[1] + quad[2]
@@ -469,15 +496,19 @@
     g = [send(full.at[core, chip], full.at[core, chip], c_s.at[j - 1], c_r.at[j - 1], 2 * j) for j in range(1, 4)]
     for copy in g:
         copy.start()
-    for copy in g:
+    e = []
+    for n, j in enumerate((0, 2, 1, 3)):
+        if j:
+            g[j - 1].wait_recv()
+        idx = flip_chip(j)
+        e.append(send(full.at[core, idx], full.at[core, idx], e_s.at[j], e_r.at[j], 1))
+        e[-1].start()
+    for copy in e:
         copy.wait_recv()
-    e = send(full.at[core], full.at[core], e_s, e_r, 1)
-    e.start()
-    e.wait_recv()
     for p in range(8):
         out_ref[:, p * width:(p + 1) * width] = full[p // 4, p % 4].astype(jnp.bfloat16)
 
-    for copy in lse_sends + d1 + [c for pair in s2 for c in pair] + s3 + [a] + b + g + [e]:
+    for copy in lse_sends + d1 + [c for pair in s2 for c in pair] + s3 + a + b + g + e:
         copy.wait_send()
 
 
@@ -516,7 +547,7 @@
             dma((2, n_chunks)), dma((2, n_chunks)),
             dma((n_chunks,)), dma((n_chunks,)),
             dma((8,)), dma((8,)),
-            dma, dma, dma((3,)), dma((3,)), dma((3,)), dma((3,)), dma, dma,
+            dma((4,)), dma((4,)), dma((3,)), dma((3,)), dma((3,)), dma((3,)), dma((4,)), dma((4,)),
         ],
         compiler_params=pltpu.CompilerParams(collective_id=0, has_side_effects=True, vmem_limit_bytes=60 * 1024 * 1024),
         name="combine",
@@ -525,16 +556,13 @@
 
 def solution(mesh):
     def local_step(hidden, ckv_blk, kpe_blk, cache_len, w_dq, q_gain, w_uq, w_dkv, kv_gain, w_uk, w_uv, w_out):
-        shard_len = ckv_blk.shape[1]
         rope = kpe_blk.shape[2]
         scale = (w_uk.shape[1] + rope) ** -0.5
-        me = lax.axis_index("sp")
         cos_t, sin_t = rope_tables(cache_len, rope)
         cos_t = jnp.concatenate([cos_t] * 4, axis=1)
         sin_t = jnp.concatenate([-sin_t, sin_t] * 2, axis=1)
         q_lat, q_pe, kv_new, c_new, k_new = project(hidden, cos_t, sin_t, w_dq, q_gain, w_uq, w_dkv.T, kv_gain, w_uk)
-        info = jnp.stack([me * shard_len, me // 2]).astype(jnp.int32)
-        ckv_out, kpe_out, o_parts, lse = attend(cache_len, info, q_lat, q_pe, c_new, k_new, ckv_blk, jnp.swapaxes(kpe_blk, 1, 2), scale)
+        ckv_out, kpe_out, o_parts, lse = attend(cache_len, q_lat, q_pe, c_new, k_new, ckv_blk, jnp.swapaxes(kpe_blk, 1, 2), scale)
         out = combine(o_parts, lse, w_uv, w_out)
         return out, ckv_out, jnp.swapaxes(kpe_out, 1, 2), kv_new
 

time: 169 us -> 160 us (0.947)
  Pallas kernels: 161 us -> 152 us
    pallas_call x1, Pallas kernels: 63.5 us -> 57.5 us  [attend(): pl.pallas_call(functools.partial(attend_kernel, n_seqs, shard_len, scale)...]
    pallas_call x1, Pallas kernels: 67 us -> 64.7 us  [combine(): pl.pallas_call(functools.partial(combine_kernel, n_seqs), out_shape=jax.S...]
where the time goes in v3:
time: 160 us; the launch traced here: 159 us
  Pallas kernels  152 us (95%)
  local copies, waits for them, and re-layouts  4.89 us (3%)
    pallas_call x1, Pallas kernels, combine(): pl.pallas_call(functools.partial(combine_kernel, n_seqs), out_shape=jax.S...  64.7 us
    pallas_call x1, Pallas kernels, attend(): pl.pallas_call(functools.partial(attend_kernel, n_seqs, shard_len, scale)...  57.5 us
    pallas_call x1, Pallas kernels, project(): pl.pallas_call(functools.partial(project_kernel, n_seqs), out_shape=[jax....  30.1 us

profile of v3, /device:TPU:0, one launch (start us, length us, event | category | flops | bytes accessed | tf_op | source)
XLA Modules:
  0.0 159.4 jit_solution(15092768913596668622)
XLA Ops:
  0.6 0.7 convert_element_type.3
  1.3 1.3 broadcast_in_dim.9.kvg_ref
  2.6 1.3 broadcast_in_dim.8.qg_ref
  3.8 0.1 fusion
  4.0 0.7 pad_maximum_fusion
  4.7 30.1 %project.1 = (bf16[2,32,64,512]{3,2,1,0:T(8,128)(2,1)}, bf16[2,32,64,64]{3,2,1,0:T(8,128)(2,1)}, bf16[32,576]{1,0:T(8,128)(2,1)}, f32[32,512]{1,0:T(8,128)}, f32[64,128]{1,0:T(8,128)}) custom-call(bf16[32,5120]{1,0:T(8,128)(2,1)} %hid_ref.1, bf16[1,1536]{1,0:T(2,128)(2,1)} %broadcast_in_dim.8.qg_ref, bf16[1,512]{1,0:T(2,128)(2,1)} %broadcast_in_dim.9.kvg_ref, ...), custom_call_target="tpu_custom_call" | custom-call | tf_op jit(solution)/shard_map/project/pallas_call | solution.py:177
  34.8 57.5 %attend.1 = (bf16[32,2048,512]{2,1,0:T(8,128)(2,1)}, bf16[32,64,2048]{2,1,0:T(8,128)(2,1)}, f32[2,4,32,16,512]{4,3,2,1,0:T(8,128)}, f32[32,128]{1,0:T(8,128)}) custom-call(s32[32]{0:T(128)} %len_ref.1, f32[32,512]{1,0:T(8,128)} %get-tuple-element.13.cnew_ref, f32[64,128]{1,0:T(8,128)} %get-tuple-element.14.knew_ref, ...), custom_call_target="tpu_custom_call" | custom-call | tf_op jit(solution)/shard_map/attend/pallas_call | solution.py:312
  92.3 0.0 copy-start
  92.3 64.7 %combine.1 = bf16[32,5120]{1,0:T(8,128)(2,1)} custom-call(f32[2,4,32,16,512]{4,3,2,1,0:T(8,128)} %get-tuple-element.17.o_hbm, f32[32,128]{1,0:T(8,128)} %get-tuple-element.18.lse_ref, bf16[128,128,512]{2,1,0:T(8,128)(2,1)} %wuv_hbm.1, bf16[16384,5120]{1,0:T(8,128)(2,1)} %wout_hbm.1), custom_call_target="tpu_custom_call" | custom-call | tf_op jit(solution)/shard_map/combine/pallas_call | solution.py:525
  157.0 1.7 %copy.18 = bf16[32,5120]{1,0:T(8,128)(2,1)} copy(bf16[32,5120]{1,0:T(8,128)(2,1)} %combine.1) | data formatting | bytes 655360
  158.7 0.0 copy-done
  158.8 0.6 copy.19
  (1 shorter events, 0.0 us)
Async XLA Ops:
  92.3 66.5 %copy-start = (bf16[32,576]{1,0:T(8,128)(2,1)S(1)}, bf16[32,576]{1,0:T(8,128)(2,1)}, u32[]{:S(2)}) copy-start(bf16[32,576]{1,0:T(8,128)(2,1)} %get-tuple-element.34) | copy-start | bytes 110596

commit v4 on v3

--- a/solution.py
+++ b/solution.py
@@ -15,7 +15,7 @@
 AHEAD = 6
 OBUF = 4
 TILE_T = 512
-CHUNK = 4
+CHUNK = 8
 
 
 def rope_tables(cache_len, rope_dim):
@@ -25,36 +25,42 @@
 
 
 def project_kernel(n_seqs, hid_ref, qg_ref, kvg_ref, cos_ref, sin_ref, wdq_hbm, wdkv_hbm, wuq_hbm, wuk_hbm,
-                   lat_hbm, pe_hbm, kv_ref, cnew_ref, knew_ref, dq_buf, dkv_buf, uq_buf, uk_buf, q_mine, q_other,
-                   lat_scr, pe_scr, lat_out, pe_out, dq_sem, dkv_sem, uq_sem, uk_sem, lo_sem, po_sem, q_s, q_r):
+                   lat_hbm, pe_hbm, kv_ref, cnew_ref, knew_ref, dq_buf, dkv_buf, uq_buf, uk_buf, cq_part, cq_got,
+                   kv_part, kv_got, q_scr, lat_buf, lat_got, pe_buf, pe_got, lat_out, pe_out,
+                   dq_sem, dkv_sem, uq_sem, uk_sem, lo_sem, po_sem, c_s, c_r, l_s, l_r, p_s, p_r):
     core = lax.rem(lax.axis_index("sp"), 2)
     partner = lax.axis_index("sp") + 1 - 2 * core
     f32, bf16 = jnp.float32, jnp.bfloat16
     n_dq, rows, q_lora = dq_buf.shape
     tile = uq_buf.shape[2]
-    n_tiles = q_mine.shape[0]
-    lat = lat_scr.shape[2]
+    n_groups, _, _, lat = lat_buf.shape
+    n_tiles = 2 * n_groups
     uq_slots = uq_buf.shape[0]
-    uk_slots = uk_buf.shape[0]
+    k_half = n_dq * rows
+    k0 = pl.multiple_of(core * k_half, 128)
 
     def uq_copy(i):
         slot = lax.rem(i, uq_slots)
         col = pl.multiple_of(core * (n_tiles * tile) + i * tile, tile)
         return pltpu.make_async_copy(wuq_hbm.at[:, pl.ds(col, tile)], uq_buf.at[slot], uq_sem.at[slot])
 
-    def uk_copy(i):
-        half = i // 4
-        head = (core + half - 2 * core * half) * 64 + lax.rem(i, 4) * 16
-        slot = lax.rem(i, uk_slots)
-        return pltpu.make_async_copy(wuk_hbm.at[pl.ds(head, 16)], uk_buf.at[slot], uk_sem.at[slot])
-
-    dq_copies = [pltpu.make_async_copy(wdq_hbm.at[pl.ds(i * rows, rows)], dq_buf.at[i], dq_sem.at[i]) for i in range(n_dq)]
-    dkv_copy = pltpu.make_async_copy(wdkv_hbm, dkv_buf, dkv_sem)
+    def uk_copy(g):
+        return pltpu.make_async_copy(wuk_hbm.at[pl.ds(core * 64 + g * 16, 16)], uk_buf.at[g], uk_sem.at[g])
+
+    def swap(src, dst, ssem, rsem):
+        return pltpu.make_async_remote_copy(src_ref=src, dst_ref=dst, send_sem=ssem, recv_sem=rsem,
+                                            device_id={"sp": partner}, device_id_type=MESH)
+
+    dq_copies = [pltpu.make_async_copy(wdq_hbm.at[pl.ds(pl.multiple_of(k0 + i * rows, 128), rows)], dq_buf.at[i], dq_sem.at[i])
+                 for i in range(n_dq)]
+    dkv_copy = pltpu.make_async_copy(wdkv_hbm.at[:, pl.ds(k0, k_half)], dkv_buf, dkv_sem)
     for copy in dq_copies:
         copy.start()
-    for i in range(uq_slots):
-        uq_copy(jnp.int32(i)).start()
     dkv_copy.start()
+    for g in range(2):
+        uq_copy(jnp.int32(2 * g)).start()
+        uq_copy(jnp.int32(2 * g + 1)).start()
+        uk_copy(jnp.int32(g)).start()
 
     barrier = pltpu.get_barrier_semaphore()
     pl.semaphore_signal(barrier, inc=1, device_id={"sp": partner}, device_id_type=MESH)
@@ -62,38 +68,23 @@
 
     def norm(v, gain):
         mean_sq = jnp.mean(v * v, axis=-1, keepdims=True)
-        return v * lax.rsqrt(mean_sq + EPS) * gain.astype(f32)
+        return v * lax.rsqrt(mean_sq + EPS) * gain
 
     acc = jnp.zeros((n_seqs, q_lora), f32)
     for i in range(n_dq):
         dq_copies[i].wait()
-        acc = acc + jnp.dot(hid_ref[:, i * rows:(i + 1) * rows], dq_buf[i], preferred_element_type=f32)
-    c_q = norm(acc, qg_ref[...]).astype(bf16)
-
-    def q_send(i):
-        return pltpu.make_async_remote_copy(src_ref=q_mine.at[i], dst_ref=q_other.at[i], send_sem=q_s.at[i], recv_sem=q_r.at[i],
-                                            device_id={"sp": partner}, device_id_type=MESH)
-
-    def q_tile(i, _):
-        uq_copy(i).wait()
-        q = jnp.dot(c_q, uq_buf[lax.rem(i, uq_slots)], preferred_element_type=f32)
-        q_mine[i] = q.astype(bf16).astype(f32)
-
-        @pl.when(i + uq_slots < n_tiles)
-        def _():
-            uq_copy(i + uq_slots).start()
-
-        @pl.when(i == n_tiles - uq_slots)
-        def _():
-            for k in range(uk_slots):
-                uk_copy(jnp.int32(k)).start()
-
-        @pl.when(i > 0)
-        def _():
-            q_send(i - 1).start()
-        return 0
-
-    lax.fori_loop(0, n_tiles, q_tile, 0)
+        hid = hid_ref[:, pl.ds(pl.multiple_of(k0 + i * rows, 128), rows)]
+        acc = acc + jnp.dot(hid, dq_buf[i], preferred_element_type=f32)
+    cq_part[...] = acc
+    cq_swap = swap(cq_part, cq_got, c_s.at[0], c_r.at[0])
+    cq_swap.start()
+    dkv_copy.wait()
+    kv_part[...] = lax.dot_general(hid_ref[:, pl.ds(k0, k_half)], dkv_buf[...], (((1,), (1,)), ((), ())), preferred_element_type=f32)
+    kv_swap = swap(kv_part, kv_got, c_s.at[1], c_r.at[1])
+    kv_swap.start()
+    cq_swap.wait_recv()
+    c_q = norm(cq_part[...] + cq_got[...], qg_ref[...]).astype(bf16)
+
     cos_t, sin_t = cos_ref[...], sin_ref[...]
     lane = lax.broadcasted_iota(jnp.int32, (n_seqs, 128), 1)
     low_half = lax.rem(lane, 64) < 32
@@ -102,9 +93,50 @@
         swapped = jnp.where(low_half, pltpu.roll(x, 96, 1), pltpu.roll(x, 32, 1))
         return x * cos_t + swapped * sin_t
 
-    dkv_copy.wait()
-    kv = lax.dot_general(hid_ref[...], dkv_buf[...], (((1,), (1,)), ((), ())), preferred_element_type=f32)
-    q_send(jnp.int32(n_tiles - 1)).start()
+    def out_copies(half, g):
+        return (pltpu.make_async_copy(lat_out.at[half, g], lat_hbm.at[half, :, pl.ds(g * 16, 16)], lo_sem.at[half, g]),
+                pltpu.make_async_copy(pe_out.at[half, g], pe_hbm.at[half, :, pl.ds(g * 16, 16)], po_sem.at[half, g]))
+
+    def swaps(g):
+        return (swap(lat_buf.at[g], lat_got.at[g], l_s.at[g], l_r.at[g]), swap(pe_buf.at[g], pe_got.at[g], p_s.at[g], p_r.at[g]))
+
+    def group(g, _):
+        for t in range(2):
+            i = 2 * g + t
+            uq_copy(i).wait()
+            q = jnp.dot(c_q, uq_buf[lax.rem(i, uq_slots)], preferred_element_type=f32)
+            q_scr[t] = q.astype(bf16).astype(f32)
+
+            @pl.when(i + uq_slots < n_tiles)
+            def _(i=i):
+                uq_copy(i + uq_slots).start()
+
+        @pl.when(g + 2 < n_groups)
+        def _():
+            uk_copy(g + 2).start()
+        uk_copy(g).wait()
+        for h in range(0, 16, 2):
+            t, p = divmod(h // 2, 4)
+            v = q_scr[t, :, p * 384:(p + 1) * 384]
+            even = v[:, :128].astype(bf16)
+            odd = pltpu.roll(v, 192, 1)[:, :128].astype(bf16)
+            rot = rotate_pairs(jnp.where(lane < 64, v[:, 128:256], v[:, 256:384]))
+            pe_buf[g, :, h, :] = rot
+            pe_buf[g, :, h + 1, :] = pltpu.roll(rot, 64, 1)
+            lat_buf[g, :, h, :] = jnp.dot(even, uk_buf[g, h], preferred_element_type=f32)
+            lat_buf[g, :, h + 1, :] = jnp.dot(odd, uk_buf[g, h + 1], preferred_element_type=f32)
+        lat_out[0, g] = lat_buf[g].astype(bf16)
+        pe_out[0, g] = pe_buf[g][:, :, :64].astype(bf16)
+        for copy in swaps(g):
+            copy.start()
+        for copy in out_copies(0, g):
+            copy.start()
+        return 0
+
+    lax.fori_loop(0, n_groups, group, 0)
+
+    kv_swap.wait_recv()
+    kv = kv_part[...] + kv_got[...]
     c_kv = norm(kv[:, :lat], kvg_ref[...]).astype(bf16)
     k_raw = jnp.concatenate([kv[:, lat:], jnp.zeros((n_seqs, 64), f32)], axis=1)
     k_pe = rotate_pairs(k_raw).astype(bf16)
@@ -114,52 +146,28 @@
     square = jnp.concatenate([k_pe.astype(f32), jnp.zeros((128 - n_seqs, 128), f32)], axis=0)
     knew_ref[...] = jnp.transpose(square)[:64, :]
 
-    def out_copies(half, g):
-        return (pltpu.make_async_copy(lat_out.at[half, g], lat_hbm.at[half, :, pl.ds(g * 16, 16)], lo_sem.at[half, g]),
-                pltpu.make_async_copy(pe_out.at[half, g], pe_hbm.at[half, :, pl.ds(g * 16, 16)], po_sem.at[half, g]))
-
-    for half in range(2):
-        src = q_mine if half == 0 else q_other
-
-        def group(g, _, half=half, src=src):
-            i = half * 4 + g
-            uk_copy(i).wait()
-            slot = lax.rem(i, uk_slots)
-            if half == 1:
-                q_send(2 * g).wait_recv()
-                q_send(2 * g + 1).wait_recv()
-            for h in range(0, 16, 2):
-                t, p = divmod(h // 2, 4)
-                v = src[2 * g + t, :, p * 384:(p + 1) * 384]
-                even = v[:, :128].astype(bf16)
-                odd = pltpu.roll(v, 192, 1)[:, :128].astype(bf16)
-                x = jnp.where(lane < 64, v[:, 128:256], v[:, 256:384])
-                rot = rotate_pairs(x)
-                pe_scr[:, h, :] = rot
-                pe_scr[:, h + 1, :] = pltpu.roll(rot, 64, 1)
-                lat_scr[:, h, :] = jnp.dot(even, uk_buf[slot, h], preferred_element_type=f32)
-                lat_scr[:, h + 1, :] = jnp.dot(odd, uk_buf[slot, h + 1], preferred_element_type=f32)
-            lat_out[half, g] = lat_scr[...].astype(bf16)
-            pe_out[half, g] = pe_scr[...][:, :, :64].astype(bf16)
-
-            @pl.when(i + uk_slots < 8)
-            def _():
-                uk_copy(i + uk_slots).start()
-            for copy in out_copies(half, g):
-                copy.start()
-            return 0
-
-        lax.fori_loop(0, 4, group, 0)
+    def receive(g, _):
+        for copy in swaps(g):
+            copy.wait_recv()
+        lat_out[1, g] = lat_got[g].astype(bf16)
+        pe_out[1, g] = pe_got[g][:, :, :64].astype(bf16)
+        for copy in out_copies(1, g):
+            copy.start()
+        return 0
+
+    lax.fori_loop(0, n_groups, receive, 0)
 
     def drain(g, _):
         for half in range(2):
             for copy in out_copies(half, g):
                 copy.wait()
-        q_send(2 * g).wait_send()
-        q_send(2 * g + 1).wait_send()
+        for copy in swaps(g):
+            copy.wait_send()
         return 0
 
-    lax.fori_loop(0, 4, drain, 0)
+    lax.fori_loop(0, n_groups, drain, 0)
+    cq_swap.wait_send()
+    kv_swap.wait_send()
 
 
 def project(hidden, cos_t, sin_t, w_dq, q_gain, w_uq, w_dkv_t, kv_gain, w_uk):
@@ -168,8 +176,8 @@
     n_heads, nope, lat = w_uk.shape
     rope = w_uq.shape[1] // n_heads - nope
     tile = 8 * (nope + rope)
-    n_tiles = n_heads // 16
-    n_dq, uq_slots, uk_slots = 8, 3, 4
+    n_groups = n_heads // 32
+    n_dq, uq_slots = 4, 4
     f32, bf16 = jnp.float32, jnp.bfloat16
     hbm = pl.BlockSpec(memory_space=pl.ANY)
     vmem = pl.BlockSpec(memory_space=pltpu.VMEM)
@@ -186,21 +194,27 @@
         in_specs=[vmem] * 5 + [hbm] * 4,
         out_specs=[hbm, hbm, vmem, vmem, vmem],
         scratch_shapes=[
-            pltpu.VMEM((n_dq, d_model // n_dq, q_lora), bf16),
-            pltpu.VMEM((lat + rope, d_model), bf16),
+            pltpu.VMEM((n_dq, d_model // (2 * n_dq), q_lora), bf16),
+            pltpu.VMEM((lat + rope, d_model // 2), bf16),
             pltpu.VMEM((uq_slots, q_lora, tile), bf16),
-            pltpu.VMEM((uk_slots, 16, nope, lat), bf16),
-            pltpu.VMEM((n_tiles, n_seqs, tile), f32),
-            pltpu.VMEM((n_tiles, n_seqs, tile), f32),
-            pltpu.VMEM((n_seqs, 16, lat), f32),
-            pltpu.VMEM((n_seqs, 16, 128), f32),
-            pltpu.VMEM((2, 4, n_seqs, 16, lat), bf16),
-            pltpu.VMEM((2, 4, n_seqs, 16, rope), bf16),
-            dma((n_dq,)), dma, dma((uq_slots,)), dma((uk_slots,)), dma((2, 4)), dma((2, 4)), dma((n_tiles,)), dma((n_tiles,)),
+            pltpu.VMEM((n_groups, 16, nope, lat), bf16),
+            pltpu.VMEM((n_seqs, q_lora), f32),
+            pltpu.VMEM((n_seqs, q_lora), f32),
+            pltpu.VMEM((n_seqs, lat + rope), f32),
+            pltpu.VMEM((n_seqs, lat + rope), f32),
+            pltpu.VMEM((2, n_seqs, tile), f32),
+            pltpu.VMEM((n_groups, n_seqs, 16, lat), f32),
+            pltpu.VMEM((n_groups, n_seqs, 16, lat), f32),
+            pltpu.VMEM((n_groups, n_seqs, 16, 128), f32),
+            pltpu.VMEM((n_groups, n_seqs, 16, 128), f32),
+            pltpu.VMEM((2, n_groups, n_seqs, 16, lat), bf16),
+            pltpu.VMEM((2, n_groups, n_seqs, 16, rope), bf16),
+            dma((n_dq,)), dma, dma((uq_slots,)), dma((n_groups,)), dma((2, n_groups)), dma((2, n_groups)), dma((2,)), dma((2,)),
+            dma((n_groups,)), dma((n_groups,)), dma((n_groups,)), dma((n_groups,)),
         ],
         compiler_params=pltpu.CompilerParams(collective_id=1, has_side_effects=True, vmem_limit_bytes=60 * 1024 * 1024),
         name="project",
-    )(hidden, q_gain[None, :], kv_gain[None, :], cos_t, sin_t, w_dq, w_dkv_t, w_uq, w_uk)
+    )(hidden, q_gain.astype(f32)[None, :], kv_gain.astype(f32)[None, :], cos_t, sin_t, w_dq, w_dkv_t, w_uq, w_uk)
 
 
 def attend_kernel(n_seqs, shard_len, scale, len_ref, cnew_ref, knew_ref, q_hbm, pe_hbm, ckv_hbm, kpe_hbm,
@@ -369,11 +383,16 @@
     head0 = core * 64 + chip * 16
     wuv_copy = pltpu.make_async_copy(wuv_hbm.at[pl.ds(head0, 16)], wuv, wt_sem.at[0])
     wout_copy = pltpu.make_async_copy(wout_hbm.at[pl.ds(pl.multiple_of(head0 * 128, 2048), 2048)], wout, wt_sem.at[1])
-    n_chunks = n_seqs // CHUNK
+    per_half = n_seqs // CHUNK
+    n_chunks = 2 * per_half
+
+    def span(c):
+        return pl.ds((c % per_half) * CHUNK, CHUNK), pl.ds((c // per_half) * 8, 8)
+
     loads = []
     for c in range(n_chunks):
-        seqs = pl.ds(c * CHUNK, CHUNK)
-        loads.append(pltpu.make_async_copy(o_hbm.at[0, :, seqs], mine.at[:, seqs], load_sem.at[c]))
+        seqs, hs = span(c)
+        loads.append(pltpu.make_async_copy(o_hbm.at[0, :, seqs, hs], mine.at[:, seqs, hs], load_sem.at[c]))
         loads[c].start()
     wuv_copy.start()
     wout_copy.start()
@@ -388,8 +407,8 @@
         copy.start()
     d1 = []
     for c in range(n_chunks):
-        seqs = pl.ds(c * CHUNK, CHUNK)
-        d1.append(send(o_hbm.at[1, :, seqs], got1.at[:, seqs], d1_s.at[c], d1_r.at[c], 1))
+        seqs, hs = span(c)
+        d1.append(send(o_hbm.at[1, :, seqs, hs], got1.at[:, seqs, hs], d1_s.at[c], d1_r.at[c], 1))
         d1[c].start()
 
     for copy in lse_sends:
@@ -414,23 +433,24 @@
     for c in range(n_chunks):
         loads[c].wait()
         d1[c].wait_recv()
+        seqs, hs = span(c)
+        head = (c // per_half) * 8
         for j in range(4):
-            row0 = pl.multiple_of(flip_chip(j) * 16, 16)
-
-            def merge(i, _, j=j, row0=row0, c=c):
-                s = c * CHUNK + i
-                wa = w_mine[s, pl.ds(row0, 16), :]
-                wb = w_part[s, pl.ds(row0, 16), :]
+            row0 = pl.multiple_of(flip_chip(j) * 16 + head, 8)
+
+            def merge(i, _, j=j, row0=row0, c=c, hs=hs):
+                s = (c % per_half) * CHUNK + i
+                wa = w_mine[s, pl.ds(row0, 8), :]
+                wb = w_part[s, pl.ds(row0, 8), :]
                 wa = jnp.concatenate([wa] * 4, axis=1)
                 wb = jnp.concatenate([wb] * 4, axis=1)
-                mine[j, s] = mine[j, s] * wa + got1[j, s] * wb
+                mine[j, s, hs] = mine[j, s, hs] * wa + got1[j, s, hs] * wb
                 return 0
 
-            lax.fori_loop(0, CHUNK, merge, 0)
+            lax.fori_loop(0, CHUNK, merge, 0, unroll=4)
         first, _ = orders(c)
-        seqs = pl.ds(c * CHUNK, CHUNK)
-        s2.append((send(mine.at[first, seqs], got2.at[0, seqs], s2_s.at[0, c], s2_r.at[0, c], 2 * first),
-                   send(mine.at[3, seqs], got2.at[1, seqs], s2_s.at[1, c], s2_r.at[1, c], 2 * first)))
+        s2.append((send(mine.at[first, seqs, hs], got2.at[0, seqs, hs], s2_s.at[0, c], s2_r.at[0, c], 2 * first),
+                   send(mine.at[3, seqs, hs], got2.at[1, seqs, hs], s2_s.at[1, c], s2_r.at[1, c], 2 * first)))
         for copy in s2[c]:
             copy.start()
 
@@ -439,40 +459,41 @@
         _, second = orders(c)
         s2[c][0].wait_recv()
         s2[c][1].wait_recv()
-
-        def add2(i, _, second=second, c=c):
-            s = c * CHUNK + i
-            mine[second, s] = mine[second, s] + got2[1, s]
-            mine[0, s] = mine[0, s] + got2[0, s]
-            return 0
-
-        lax.fori_loop(0, CHUNK, add2, 0)
-        seqs = pl.ds(c * CHUNK, CHUNK)
-        s3.append(send(mine.at[second, seqs], got3.at[seqs], s3_s.at[c], s3_r.at[c], 2 * second))
+        seqs, hs = span(c)
+        mine[second, seqs, hs] = mine[second, seqs, hs] + got2[1, seqs, hs]
+        s3.append(send(mine.at[second, seqs, hs], got3.at[seqs, hs], s3_s.at[c], s3_r.at[c], 2 * second))
+        mine[0, seqs, hs] = mine[0, seqs, hs] + got2[0, seqs, hs]
         s3[c].start()
 
-    for c in range(n_chunks):
+    def latents(c):
         s3[c].wait_recv()
-
-        def add3(i, _, c=c):
-            s = c * CHUNK + i
-            mine[0, s] = mine[0, s] + got3[s]
-            return 0
-
-        lax.fori_loop(0, CHUNK, add3, 0)
-
+        seqs, hs = span(c)
+        mine[0, seqs, hs] = mine[0, seqs, hs] + got3[seqs, hs]
+
+    def value_heads(h0):
+        for h in range(h0, h0 + 8):
+            x = mine[0, :, h, :].astype(jnp.bfloat16)
+            o = lax.dot_general(x, wuv[h], (((1,), (1,)), ((), ())), preferred_element_type=jnp.float32)
+            heads[:, h * 128:(h + 1) * 128] = o.astype(jnp.bfloat16)
+
+    width = wout.shape[1] // 8
+    depth = wout.shape[0] // 2
+
+    for c in range(per_half):
+        latents(c)
     wuv_copy.wait()
-    for h in range(16):
-        x = mine[0, :, h, :].astype(jnp.bfloat16)
-        o = lax.dot_general(x, wuv[h], (((1,), (1,)), ((), ())), preferred_element_type=jnp.float32)
-        heads[:, h * 128:(h + 1) * 128] = o.astype(jnp.bfloat16)
+    value_heads(0)
     wout_copy.wait()
-    width = wout.shape[1] // 8
+    for p in range(8):
+        part[p // 4, p % 4] = jnp.dot(heads[:, :depth], wout[:depth, p * width:(p + 1) * width], preferred_element_type=jnp.float32)
+    for c in range(per_half, n_chunks):
+        latents(c)
+    value_heads(8)
 
     def project_block(which, order):
         idx = flip_chip(order)
         col = pl.multiple_of((which * 4 + idx) * width, 128)
-        part[which, idx] = jnp.dot(heads[...], wout[:, pl.ds(col, width)], preferred_element_type=jnp.float32)
+        part[which, idx] = part[which, idx] + jnp.dot(heads[:, depth:], wout[depth:, pl.ds(col, width)], preferred_element_type=jnp.float32)
 
     a = []
     for j in (3, 1, 2, 0):
@@ -516,7 +537,7 @@
     _, _, n_seqs, _, lat = o_parts.shape
     d_model = w_out.shape[1]
     vdim = w_uv.shape[1]
-    n_chunks = n_seqs // CHUNK
+    n_chunks = 2 * n_seqs // CHUNK
     width = d_model // 8
     hbm = pl.BlockSpec(memory_space=pl.ANY)
     vmem = pl.BlockSpec(memory_space=pltpu.VMEM)

time: 160 us -> 154 us (0.963)
  Pallas kernels: 152 us -> 146 us
    pallas_call x1, Pallas kernels: 30.1 us -> 26.6 us  [project(): pl.pallas_call(functools.partial(project_kernel, n_seqs), out_shape=[jax....]
    pallas_call x1, Pallas kernels: 64.7 us -> 62.3 us  [combine(): pl.pallas_call(functools.partial(combine_kernel, n_seqs), out_shape=jax.S...]
where the time goes in v4:
time: 154 us; the launch traced here: 153 us
  Pallas kernels  146 us (95%)
  local copies, waits for them, and re-layouts  3.62 us (2%)
  other arithmetic  2.78 us (2%)
    pallas_call x1, Pallas kernels, combine(): pl.pallas_call(functools.partial(combine_kernel, n_seqs), out_shape=jax.S...  62.3 us
    pallas_call x1, Pallas kernels, attend(): pl.pallas_call(functools.partial(attend_kernel, n_seqs, shard_len, scale)...  57.5 us
    pallas_call x1, Pallas kernels, project(): pl.pallas_call(functools.partial(project_kernel, n_seqs), out_shape=[jax....  26.6 us

profile of v4, /device:TPU:0, one launch (start us, length us, event | category | flops | bytes accessed | tf_op | source)
XLA Modules:
  0.0 153.4 jit_solution(6197735924468156089)
XLA Ops:
  0.6 0.7 convert_element_type.2
  1.3 1.3 broadcast_in_dim.17
  2.6 1.3 reshape.14.qg_ref
  3.8 0.1 fusion
  4.0 0.7 pad_maximum_fusion
  4.7 26.6 %project.1 = (bf16[2,32,64,512]{3,2,1,0:T(8,128)(2,1)}, bf16[2,32,64,64]{3,2,1,0:T(8,128)(2,1)}, bf16[32,576]{1,0:T(8,128)(2,1)}, f32[32,512]{1,0:T(8,128)}, f32[64,128]{1,0:T(8,128)}) custom-call(bf16[32,5120]{1,0:T(8,128)(2,1)} %hid_ref.1, f32[1,1536]{1,0:T(1,128)} %reshape.14.qg_ref, f32[1,512]{1,0:T(1,128)} %bitcast.6, ...), custom_call_target="tpu_custom_call" | custom-call | tf_op jit(solution)/shard_map/project/pallas_call | solution.py:185
  31.3 57.5 %attend.1 = (bf16[32,2048,512]{2,1,0:T(8,128)(2,1)}, bf16[32,64,2048]{2,1,0:T(8,128)(2,1)}, f32[2,4,32,16,512]{4,3,2,1,0:T(8,128)}, f32[32,128]{1,0:T(8,128)}) custom-call(s32[32]{0:T(128)} %len_ref.1, f32[32,512]{1,0:T(8,128)} %get-tuple-element.13.cnew_ref, f32[64,128]{1,0:T(8,128)} %get-tuple-element.14.knew_ref, ...), custom_call_target="tpu_custom_call" | custom-call | tf_op jit(solution)/shard_map/attend/pallas_call | solution.py:326
  88.8 0.0 copy-start
  88.8 62.3 %combine.1 = bf16[32,5120]{1,0:T(8,128)(2,1)} custom-call(f32[2,4,32,16,512]{4,3,2,1,0:T(8,128)} %get-tuple-element.17.o_hbm, f32[32,128]{1,0:T(8,128)} %get-tuple-element.18.lse_ref, bf16[128,128,512]{2,1,0:T(8,128)(2,1)} %wuv_hbm.1, bf16[16384,5120]{1,0:T(8,128)(2,1)} %wout_hbm.1), custom_call_target="tpu_custom_call" | custom-call | tf_op jit(solution)/shard_map/combine/pallas_call | solution.py:546
  151.1 1.7 %copy.18 = bf16[32,5120]{1,0:T(8,128)(2,1)} copy(bf16[32,5120]{1,0:T(8,128)(2,1)} %combine.1) | data formatting | bytes 655360
  152.8 0.0 copy-done
  152.8 0.6 copy.19
  (1 shorter events, 0.0 us)
Async XLA Ops:
  88.8 64.0 %copy-start = (bf16[32,576]{1,0:T(8,128)(2,1)S(1)}, bf16[32,576]{1,0:T(8,128)(2,1)}, u32[]{:S(2)}) copy-start(bf16[32,576]{1,0:T(8,128)(2,1)} %get-tuple-element.34) | copy-start | bytes 110596

commit v5 on v4

--- a/solution.py
+++ b/solution.py
@@ -68,7 +68,7 @@
 
     def norm(v, gain):
         mean_sq = jnp.mean(v * v, axis=-1, keepdims=True)
-        return v * lax.rsqrt(mean_sq + EPS) * gain
+        return v * lax.rsqrt(mean_sq + EPS) * gain.astype(f32)[None, :]
 
     acc = jnp.zeros((n_seqs, q_lora), f32)
     for i in range(n_dq):
@@ -99,6 +99,25 @@
 
     def swaps(g):
         return (swap(lat_buf.at[g], lat_got.at[g], l_s.at[g], l_r.at[g]), swap(pe_buf.at[g], pe_got.at[g], p_s.at[g], p_r.at[g]))
+
+    kv_swap.wait_recv()
+    kv = kv_part[...] + kv_got[...]
+    c_kv = norm(kv[:, :lat], kvg_ref[...]).astype(bf16)
+    k_raw = jnp.concatenate([kv[:, lat:], jnp.zeros((n_seqs, 64), f32)], axis=1)
+    k_pe = rotate_pairs(k_raw).astype(bf16)
+    kv_ref[:, :lat] = c_kv
+    kv_ref[:, lat:] = k_pe[:, :64]
+    cnew_ref[...] = c_kv.astype(f32)
+    square = jnp.concatenate([k_pe.astype(f32), jnp.zeros((128 - n_seqs, 128), f32)], axis=0)
+    knew_ref[...] = jnp.transpose(square)[:64, :]
+
+    def receive(g):
+        for copy in swaps(g):
+            copy.wait_recv()
+        lat_out[1, g] = lat_got[g].astype(bf16)
+        pe_out[1, g] = pe_got[g][:, :, :64].astype(bf16)
+        for copy in out_copies(1, g):
+            copy.start()
 
     def group(g, _):
         for t in range(2):
@@ -131,31 +150,15 @@
             copy.start()
         for copy in out_copies(0, g):
             copy.start()
+
+        @pl.when(g >= 1)
+        def _():
+            receive(g - 1)
         return 0
 
     lax.fori_loop(0, n_groups, group, 0)
 
-    kv_swap.wait_recv()
-    kv = kv_part[...] + kv_got[...]
-    c_kv = norm(kv[:, :lat], kvg_ref[...]).astype(bf16)
-    k_raw = jnp.concatenate([kv[:, lat:], jnp.zeros((n_seqs, 64), f32)], axis=1)
-    k_pe = rotate_pairs(k_raw).astype(bf16)
-    kv_ref[:, :lat] = c_kv
-    kv_ref[:, lat:] = k_pe[:, :64]
-    cnew_ref[...] = c_kv.astype(f32)
-    square = jnp.concatenate([k_pe.astype(f32), jnp.zeros((128 - n_seqs, 128), f32)], axis=0)
-    knew_ref[...] = jnp.transpose(square)[:64, :]
-
-    def receive(g, _):
-        for copy in swaps(g):
-            copy.wait_recv()
-        lat_out[1, g] = lat_got[g].astype(bf16)
-        pe_out[1, g] = pe_got[g][:, :, :64].astype(bf16)
-        for copy in out_copies(1, g):
-            copy.start()
-        return 0
-
-    lax.fori_loop(0, n_groups, receive, 0)
+    receive(n_groups - 1)
 
     def drain(g, _):
         for half in range(2):
@@ -214,11 +217,11 @@
         ],
         compiler_params=pltpu.CompilerParams(collective_id=1, has_side_effects=True, vmem_limit_bytes=60 * 1024 * 1024),
         name="project",
-    )(hidden, q_gain.astype(f32)[None, :], kv_gain.astype(f32)[None, :], cos_t, sin_t, w_dq, w_dkv_t, w_uq, w_uk)
-
-
-def attend_kernel(n_seqs, shard_len, scale, len_ref, cnew_ref, knew_ref, q_hbm, pe_hbm, ckv_hbm, kpe_hbm,
-                  ckv_out, kpe_out, o_hbm, lse_ref, cbuf, kbuf, qbuf, pbuf, obuf, s_scr, lse_scr, in_sem, out_sem, o_sem):
+    )(hidden, q_gain, kv_gain, cos_t, sin_t, w_dq, w_dkv_t, w_uq, w_uk)
+
+
+def attend_kernel(n_seqs, shard_len, scale, len_ref, cnew_ref, knew_ref, kv_ref, q_hbm, pe_hbm, ckv_hbm, kpe_hbm,
+                  ckv_out, kpe_out, o_hbm, lse_ref, kv_out, cbuf, kbuf, qbuf, pbuf, obuf, s_scr, lse_scr, in_sem, out_sem, o_sem):
     step = pl.program_id(0)
     me = lax.axis_index("sp")
     chip = me // 2
@@ -311,6 +314,7 @@
     @pl.when(step == n_seqs - 1)
     def _():
         lse_ref[...] = jnp.transpose(lse_scr[...])[:n_seqs, :]
+        kv_out[...] = kv_ref[...]
         for seq in range(n_seqs - NBUF, n_seqs):
             for copy in copies_out(jnp.int32(seq)):
                 copy.wait()
@@ -318,7 +322,7 @@
             copy_o(jnp.int32(seq)).wait()
 
 
-def attend(cache_len, q_lat, q_pe, c_new, k_new, ckv, kpe_t, scale):
+def attend(cache_len, q_lat, q_pe, c_new, k_new, kv_new, ckv, kpe_t, scale):
     n_seqs, shard_len, lat = ckv.shape
     rope = kpe_t.shape[1]
     whole = lambda shape: pl.BlockSpec(shape, lambda i, *_: (0,) * len(shape))
@@ -328,8 +332,8 @@
         grid_spec=pltpu.PrefetchScalarGridSpec(
             num_scalar_prefetch=1,
             grid=(n_seqs,),
-            in_specs=[whole((n_seqs, lat)), whole((rope, 128)), hbm, hbm, hbm, hbm],
-            out_specs=[hbm, hbm, hbm, whole((n_seqs, 128))],
+            in_specs=[whole((n_seqs, lat)), whole((rope, 128)), whole(kv_new.shape), hbm, hbm, hbm, hbm],
+            out_specs=[hbm, hbm, hbm, whole((n_seqs, 128)), whole(kv_new.shape)],
             scratch_shapes=[
                 pltpu.VMEM((NBUF, shard_len, lat), jnp.bfloat16),
                 pltpu.VMEM((NBUF, rope, shard_len), jnp.bfloat16),
@@ -348,10 +352,11 @@
             jax.ShapeDtypeStruct(kpe_t.shape, kpe_t.dtype),
             jax.ShapeDtypeStruct((2, 4, n_seqs, 16, lat), jnp.float32),
             jax.ShapeDtypeStruct((n_seqs, 128), jnp.float32),
+            jax.ShapeDtypeStruct(kv_new.shape, kv_new.dtype),
         ],
         compiler_params=pltpu.CompilerParams(dimension_semantics=("arbitrary",), vmem_limit_bytes=60 * 1024 * 1024),
         name="attend",
-    )(cache_len, c_new, k_new, q_lat, q_pe, ckv, kpe_t)
+    )(cache_len, c_new, k_new, kv_new, q_lat, q_pe, ckv, kpe_t)
 
 
 def combine_kernel(n_seqs, o_hbm, lse_ref, wuv_hbm, wout_hbm, out_ref, mine, got1, got2, got3, lse_all, w_mine, w_part,
@@ -394,8 +399,6 @@
         seqs, hs = span(c)
         loads.append(pltpu.make_async_copy(o_hbm.at[0, :, seqs, hs], mine.at[:, seqs, hs], load_sem.at[c]))
         loads[c].start()
-    wuv_copy.start()
-    wout_copy.start()
 
     barrier = pltpu.get_barrier_semaphore()
     for bits in range(1, 8):
@@ -453,6 +456,9 @@
                    send(mine.at[3, seqs, hs], got2.at[1, seqs, hs], s2_s.at[1, c], s2_r.at[1, c], 2 * first)))
         for copy in s2[c]:
             copy.start()
+
+    wuv_copy.start()
+    wout_copy.start()
 
     s3 = []
     for c in range(n_chunks):
@@ -583,7 +589,7 @@
         cos_t = jnp.concatenate([cos_t] * 4, axis=1)
         sin_t = jnp.concatenate([-sin_t, sin_t] * 2, axis=1)
         q_lat, q_pe, kv_new, c_new, k_new = project(hidden, cos_t, sin_t, w_dq, q_gain, w_uq, w_dkv.T, kv_gain, w_uk)
-        ckv_out, kpe_out, o_parts, lse = attend(cache_len, q_lat, q_pe, c_new, k_new, ckv_blk, jnp.swapaxes(kpe_blk, 1, 2), scale)
+        ckv_out, kpe_out, o_parts, lse, kv_new = attend(cache_len, q_lat, q_pe, c_new, k_new, kv_new, ckv_blk, jnp.swapaxes(kpe_blk, 1, 2), scale)
         out = combine(o_parts, lse, w_uv, w_out)
         return out, ckv_out, jnp.swapaxes(kpe_out, 1, 2), kv_new
 

time: 154 us -> 152 us (0.987)
  Pallas kernels: 146 us -> 148 us
  local copies, waits for them, and re-layouts: 3.62 us -> 1.72 us
where the time goes in v5:
time: 152 us
  Pallas kernels  148 us (97%)
  local copies, waits for them, and re-layouts  1.72 us (1%)
  other arithmetic  1.53 us (1%)
    pallas_call x1, Pallas kernels, combine(): pl.pallas_call(functools.partial(combine_kernel, n_seqs), out_shape=jax.S...  62.3 us
    pallas_call x1, Pallas kernels, attend(): pl.pallas_call(functools.partial(attend_kernel, n_seqs, shard_len, scale)...  57.7 us
    pallas_call x1, Pallas kernels, project(): pl.pallas_call(functools.partial(project_kernel, n_seqs), out_shape=[jax....  28.1 us

profile of v5, /device:TPU:0, one launch (start us, length us, event | category | flops | bytes accessed | tf_op | source)
XLA Modules:
  0.0 152.0 jit_solution(12183054522349218875)
XLA Ops:
  0.6 0.7 convert_element_type.3
  1.3 0.1 fusion
  1.5 0.7 pad_maximum_fusion
  2.2 28.1 %project.1 = (bf16[2,32,64,512]{3,2,1,0:T(8,128)(2,1)}, bf16[2,32,64,64]{3,2,1,0:T(8,128)(2,1)}, bf16[32,576]{1,0:T(8,128)(2,1)}, f32[32,512]{1,0:T(8,128)}, f32[64,128]{1,0:T(8,128)}) custom-call(bf16[32,5120]{1,0:T(8,128)(2,1)} %hid_ref.1, bf16[1536]{0:T(1024)(128)(2,1)} %qg_ref.1, bf16[512]{0:T(512)(128)(2,1)} %kvg_ref.1, ...), custom_call_target="tpu_custom_call" | custom-call | tf_op jit(solution)/shard_map/project/pallas_call | solution.py:188
  30.2 57.7 %attend.1 = (bf16[32,2048,512]{2,1,0:T(8,128)(2,1)}, bf16[32,64,2048]{2,1,0:T(8,128)(2,1)}, f32[2,4,32,16,512]{4,3,2,1,0:T(8,128)}, f32[32,128]{1,0:T(8,128)}, bf16[32,576]{1,0:T(8,128)(2,1)}) custom-call(s32[32]{0:T(128)} %len_ref.1, f32[32,512]{1,0:T(8,128)} %get-tuple-element.14.cnew_ref, f32[64,128]{1,0:T(8,128)} %get-tuple-element.15.knew_ref, ...), custom_call_target="tpu_custom_call" | custom-call | tf_op jit(solution)/shard_map/attend/pallas_call | solution.py:330
  87.9 62.3 %combine.1 = bf16[32,5120]{1,0:T(8,128)(2,1)} custom-call(f32[2,4,32,16,512]{4,3,2,1,0:T(8,128)} %get-tuple-element.19.o_hbm, f32[32,128]{1,0:T(8,128)} %get-tuple-element.20.lse_ref, bf16[128,128,512]{2,1,0:T(8,128)(2,1)} %wuv_hbm.1, bf16[16384,5120]{1,0:T(8,128)(2,1)} %wout_hbm.1), custom_call_target="tpu_custom_call" | custom-call | tf_op jit(solution)/shard_map/combine/pallas_call | solution.py:552
  150.3 1.7 %copy.17 = bf16[32,5120]{1,0:T(8,128)(2,1)} copy(bf16[32,5120]{1,0:T(8,128)(2,1)} %combine.1) | data formatting | bytes 655360
  (1 shorter events, 0.0 us)
